TPU v7x, 256 devices: a whole 4x4x8 slice. The times are simulated.
256 devices in a mesh: row: 32 (over z, x), col: 8 (over y, core).
Axes of the slice: x: 4, y: 4, z: 8, core: 2. Of those that a mesh axis runs over, the one named last changes fastest.
Arguments:
- factor: float32 [9, 1024, 3, 1024], P(None, 'row', None, 'col'), may hold values from -2 to 2.5, as said below
- adjoint: float32 [9, 1024, 3, 1024], P(None, 'row', None, 'col'), may hold values from -6 to 6
Outputs:
- kernel_adjoint: float32 [9, 1024, 3, 1024], P(None, 'row', None, 'col')
Inputs may be any that keep to these rules, and one draw needn't show every extreme that they name: `factor`: zero where the column minus 2048 exceeds the row; the diagonal entries of the two 512-square diagonal blocks lie between 1 and 2.5.
All inputs are finite; a program needn't handle non-finite values.
Results may differ from a plain program's by a relative error of at most 0.0001.
Values sent between devices are 32-bit elements; how exact they have to be, the bound alone decides.
No kernel may reach another device: no remote copies, remote signals or barrier semaphores. Data moves between devices by JAX's collectives and lax.ppermute only.
A program may use at most 64 MiB of HBM per device.

v0:
```python
import jax
import jax.numpy as jnp
from jax import lax
from jax.sharding import Mesh
from jax.sharding import PartitionSpec as P

NB = 512
ROW = ("row_0", "row_1")


def joined_along(blocks, dim):
    lengths = list(blocks.shape[1:])
    lengths[dim] *= blocks.shape[0]
    return jnp.moveaxis(blocks, 0, dim).reshape(lengths)


def sent_to_all(array, axis):
    size = lax.axis_size(axis)
    return lax.all_to_all(
        jnp.broadcast_to(array[None], (size, *array.shape)), axis, 0, 0, tiled=True
    )


def gathered_copies(array, axis, dim):
    return joined_along(sent_to_all(array, axis), dim)


def sent_together(arrays, axis, dim, along):
    ends, at = ([], 0)
    for a in arrays[:-1]:
        at += a.shape[along]
        ends.append(at)
    both = jnp.concatenate(arrays, axis=along)
    return tuple(jnp.split(lax.all_gather(both, axis, axis=dim, tiled=True), ends, axis=along))


def rows_for(lines, size):
    spare = -len(lines) % size
    return jnp.pad(lines, [(0, spare)] + [(0, 0)] * (lines.ndim - 1))


def own_block(blocks, axes, order):
    lengths = [lax.axis_size(a) for a in axes]
    blocks = blocks.reshape(*lengths, *blocks.shape[1:])
    blocks = blocks.transpose(*order, *range(len(axes), blocks.ndim))
    blocks = blocks.reshape(-1, *blocks.shape[len(axes) :])
    for k in order:
        blocks = lax.psum_scatter(blocks, axes[k], scatter_dimension=0, tiled=True)
    return blocks[0]


def all_blocks(array, axes, order):
    blocks = array[None]
    for k in order:
        blocks = lax.all_gather(blocks, axes[k], axis=0, tiled=True)
    block = [lax.axis_size(axes[k]) for k in reversed(order)]
    blocks = blocks.reshape(*block, *array.shape)
    turned = sorted(range(len(order)), key=lambda place: order[len(order) - 1 - place])
    return blocks.transpose(*turned, *range(len(order), blocks.ndim)).reshape(-1, *array.shape)


def sum_by_parts(array, axes, order):
    size, lines = (lax.axis_size(axes), array.reshape(-1, *array.shape[1:][-1:]))
    blocks = rows_for(lines, size).reshape(size, -1, *lines.shape[1:])
    own = own_block(blocks, axes, order)
    whole = all_blocks(own, axes, order[::-1]).reshape(-1, *lines.shape[1:])
    return whole[: len(lines)].reshape(array.shape)


def cut_along(array, dim, size):
    lengths = array.shape
    blocks = array.reshape(*lengths[:dim], size, lengths[dim] // size, *lengths[dim + 1 :])
    return jnp.moveaxis(blocks, dim, 0)


def sent_and_summed(array, axis, dim):
    blocks = cut_along(array, dim, lax.axis_size(axis))
    arrived = lax.all_to_all(blocks, axis, split_axis=0, concat_axis=0, tiled=True)
    return arrived.sum(axis=0)


def swapped(array, axis, apart):
    return lax.ppermute(array, axis, [(i, i ^ 1 << apart) for i in range(lax.axis_size(axis))])


def exact_dot(first, second):
    return jnp.dot(
        first, second, precision=lax.Precision.HIGHEST, preferred_element_type=jnp.float32
    )


def lower_half(matrix):
    return jnp.tril(matrix) - 0.5 * jnp.diag(jnp.diag(matrix))


def local(factor, adjoint):
    row_cycles, tile_rows, col_cycles, tile_cols = factor.shape
    col_devices = lax.axis_size("col")
    row_devices = lax.axis_size(ROW)
    row_span = tile_rows * row_devices
    col_span = tile_cols * col_devices
    row_index = lax.axis_index(ROW)
    col_index = lax.axis_index("col")
    local_rows = row_cycles * tile_rows
    local_cols = col_cycles * tile_cols
    left_cols = col_cycles * col_span - 2 * NB
    panel_cycles = 2 * NB // col_span
    row_blocks = 2 * NB // row_span
    owned_rows = row_blocks * tile_rows
    owned_cols = panel_cycles * tile_cols
    split_col = local_cols - owned_cols
    row_steps = jnp.arange(local_rows, dtype=jnp.int32)
    col_steps = jnp.arange(local_cols, dtype=jnp.int32)
    global_rows = row_steps // tile_rows * row_span + row_index * tile_rows + row_steps % tile_rows
    global_cols = col_steps // tile_cols * col_span + col_index * tile_cols + col_steps % tile_cols
    factor_flat = factor.reshape(local_rows, local_cols)
    working = jnp.where(
        global_cols[None, :] - left_cols > global_rows[:, None],
        0.0,
        adjoint.reshape(local_rows, local_cols),
    )
    factor_local = factor_flat[:, split_col:].reshape(local_rows, panel_cycles, tile_cols)
    factor_panels = gathered_copies(factor_local, "col", 2).reshape(local_rows, 2 * NB)
    factor_tops = factor_flat[:owned_rows].reshape(row_blocks, tile_rows, local_cols)
    diag_part = factor_panels[:owned_rows].reshape(row_blocks, tile_rows, 2 * NB)
    top_rows, diag_full = sent_together((factor_tops, diag_part), ROW, 1, 2)
    top_rows = top_rows.reshape(2 * NB, local_cols)
    diag_full = diag_full.reshape(2 * NB, 2 * NB)
    owned_global = global_rows[:owned_rows]
    block_ids = jnp.arange(NB, dtype=jnp.int32)
    panel_globals = global_cols[split_col:]
    first_row = NB
    bottom = first_row + NB
    first_col = left_cols + first_row
    beneath = (global_rows >= bottom)[:, None]
    col_left = (global_cols < first_col)[None, :]
    adjoint_local = working[:, split_col:].reshape(local_rows, panel_cycles, tile_cols)
    adjoint_panels = gathered_copies(adjoint_local, "col", 2).reshape(local_rows, 2 * NB)
    diag_block = diag_full[first_row:bottom, first_row:bottom]
    panel_factor = jnp.where(beneath, factor_panels[:, first_row:bottom], 0.0)
    solved_cols = lax.linalg.triangular_solve(
        diag_block, adjoint_panels[:, first_row:bottom], left_side=False, lower=True
    )
    column_adjoint = jnp.where(beneath, solved_cols, 0.0)
    picker = (owned_global[None, :] == first_row + block_ids[:, None]).astype(jnp.float32)
    partial_sum = exact_dot(picker, adjoint_panels[:owned_rows, first_row:bottom]) - jnp.tril(
        exact_dot(column_adjoint.T, panel_factor)
    )
    diag_start = sum_by_parts(partial_sum, ROW, (0, 1))
    product = lower_half(exact_dot(diag_block.T, diag_start))
    left_solved = lax.linalg.triangular_solve(
        diag_block, product, left_side=True, lower=True, transpose_a=True
    )
    symmetric = lax.linalg.triangular_solve(diag_block, left_solved, left_side=False, lower=True)
    diag_adjoint = lower_half(symmetric + symmetric.T)
    owned_sym = exact_dot(picker.T, diag_adjoint + diag_adjoint.T)
    panel_rows_l = top_rows[first_row:bottom]
    trail_update = exact_dot(column_adjoint, panel_rows_l)
    row_extra = exact_dot(owned_sym, panel_rows_l)
    trail_factor = jnp.where(beneath & col_left, factor_flat, 0.0)
    half_devices = row_devices // 2
    share_rows = tile_rows // 2
    grouped = column_adjoint.reshape(local_rows, half_devices, 2, share_rows).transpose(0, 2, 1, 3)
    grouped = grouped[:, ::-1]
    ordered = grouped.reshape(local_rows, NB)
    own_share = sent_and_summed(exact_dot(ordered.T, trail_factor), ROW, 0)
    partner_share = swapped(own_share, ROW, row_devices.bit_length() - 2)
    summed = jnp.concatenate([own_share, partner_share], 0)
    in_panel = ((owned_global >= first_row) & (owned_global < bottom))[:, None]
    row_change = jnp.where(in_panel & col_left, summed + row_extra, 0.0)
    working = working - jnp.where(beneath & col_left, trail_update, 0.0)
    working = jnp.concatenate([working[:owned_rows] - row_change, working[owned_rows:]], 0)
    owned_diag = exact_dot(picker.T, diag_adjoint)
    new_slot = jnp.where(beneath, column_adjoint, adjoint_panels[:, first_row:bottom])
    new_slot = jnp.concatenate(
        [jnp.where(in_panel, owned_diag, new_slot[:owned_rows]), new_slot[owned_rows:]], 0
    )
    new_panels = jnp.concatenate(
        [adjoint_panels[:, :first_row], new_slot, adjoint_panels[:, bottom:]], 1
    )
    local_new = lax.dynamic_index_in_dim(
        new_panels.reshape(local_rows, panel_cycles, col_devices, tile_cols),
        col_index,
        2,
        keepdims=False,
    ).reshape(local_rows, owned_cols)
    in_cols = ((panel_globals >= first_col) & (panel_globals < first_col + NB))[None, :]
    working = jnp.concatenate(
        [working[:, :split_col], jnp.where(in_cols, local_new, working[:, split_col:])], 1
    )
    return working.reshape(row_cycles, tile_rows, col_cycles, tile_cols)


def solution(mesh):
    split = Mesh(mesh.devices.reshape(8, 4, mesh.shape["col"]), ("row_0", "row_1", "col"))
    placed = (P(None, ROW, None, "col"), P(None, ROW, None, "col"))
    return jax.shard_map(
        local, mesh=split, in_specs=placed, out_specs=P(None, ROW, None, "col"), check_vma=False
    )
```

profile of v0, /device:TPU:4, one launch (start us, length us, event | category | flops | bytes accessed | tf_op | source)
XLA Modules:
  0.0 331.9 jit_solution(6337238052615633876)
XLA Ops:
  6.5 1.3 copy.23
  7.9 1.1 broadcast_in_dim.111
  9.0 4.5 %all-to-all-start.1 = ((f32[8,288,1,128]{3,1,2,0:T(8,128)}), f32[8,288,1,128]{3,1,2,0:T(8,128)S(1)}, u32[]{:S(2)}, u32[]{:S(2)}) async-start(f32[8,288,1,128]{3,1,2,0:T(8,128)} %broadcast_in_dim.111), calls=%async_computation.1 | async-start | bytes 2359296 | tf_op jit(solution)/shard_map/all_to_all | solution.py:19
  13.6 0.8 copy_bitcast_fusion.3
  14.4 16.4 %all-to-all-done.1 = f32[8,288,1,128]{3,1,2,0:T(8,128)S(1)} async-done(((f32[8,288,1,128]{3,1,2,0:T(8,128)}), f32[8,288,1,128]{3,1,2,0:T(8,128)S(1)}, u32[]{:S(2)}, u32[]{:S(2)}) %all-to-all-start.1) | async-done | bytes 1179680 | tf_op jit(solution)/shard_map/all_to_all | solution.py:19
  32.2 1.1 broadcast_in_dim.110
  33.4 3.6 %all-to-all-start = ((f32[8,288,1,128]{3,1,2,0:T(8,128)}), f32[8,288,1,128]{3,1,2,0:T(8,128)S(1)}, u32[]{:S(2)}, u32[]{:S(2)}) async-start(f32[8,288,1,128]{3,1,2,0:T(8,128)} %broadcast_in_dim.110), calls=%async_computation | async-start | bytes 2359296 | tf_op jit(solution)/shard_map/all_to_all | solution.py:19
  37.0 1.7 copy.31
  38.8 15.4 %all-to-all-done = f32[8,288,1,128]{3,1,2,0:T(8,128)S(1)} async-done(((f32[8,288,1,128]{3,1,2,0:T(8,128)}), f32[8,288,1,128]{3,1,2,0:T(8,128)S(1)}, u32[]{:S(2)}, u32[]{:S(2)}) %all-to-all-start) | async-done | bytes 1179680 | tf_op jit(solution)/shard_map/all_to_all | solution.py:19
  55.1 1.0 copy-done.1
  56.1 1.2 copy.46
  57.4 60.4 %all-gather.3.cloned.1.call-done = f32[1,1024,1408]{2,1,0:T(8,128)} async-done(((f32[1,32,1408]{2,1,0:T(8,128)}), f32[1,1024,1408]{2,1,0:T(8,128)}) %all-gather.3.cloned.1.call-update) | async-done | bytes 5767184 | tf_op jit(solution)/shard_map/all_gather | solution.py:34
  117.7 2.5 slice_bitcast_fusion
  120.2 2.0 copy-done
  122.4 10.2 %while.1 = (s32[]{:T(128)}, f32[512,512]{1,0:T(8,128)S(1)}, s32[4,2]{0,1:T(2,128)S(1)}, f32[4,128,128]{2,1,0:T(8,128)}, s32[]{:T(128)}) while((s32[]{:T(128)}, f32[512,512]{1,0:T(8,128)S(1)}, s32[4,2]{0,1:T(2,128)S(1)}, f32[4,128,128]{2,1,0:T(8,128)}, s32[]{:T(128)}) %tuple.20), condition=%wide.while_cond, body=%wide.while_body.sunk | while | flops 2 | bytes 132705 | solution.py:141
  123.1 1.9 bitcast_dynamic-update-slice_fusion.2
  125.6 1.9 bitcast_dynamic-update-slice_fusion.2
  128.2 1.9 bitcast_dynamic-update-slice_fusion.2
  130.7 1.9 bitcast_dynamic-update-slice_fusion.2
  132.6 40.1 %custom-call.7 = f32[4,128,128]{1,2,0:T(8,128)S(1)} custom-call(f32[4,128,128]{2,1,0:T(8,128)} %get-tuple-element.12), custom_call_target="InvertDiagBlocksLowerTriangular" | custom-call | tf_op jit(solution)/shard_map/triangular_solve | solution.py:141
  175.2 2.1 convolution_select_fusion
  177.3 1.6 convolution_subtract_fusion
  179.0 37.4 %reduce-scatter.3.cloned.1.call-done = f32[4,16,512]{2,1,0:T(8,128)} async-done(((f32[32,16,512]{2,1,0:T(8,128)}), f32[4,16,512]{2,1,0:T(8,128)}) %reduce-scatter.3.cloned.1.call-update) | async-done | bytes 131088 | tf_op jit(solution)/shard_map/reduce_scatter | solution.py:48
  217.1 1.0 reshape.199
  218.1 0.8 copy.25
  218.9 0.8 copy.26
  221.3 17.9 %reduce-scatter.5.cloned.1.call-done = f32[1,16,512]{2,1,0:T(8,128)} async-done(((f32[4,16,512]{2,1,0:T(8,128)}), f32[1,16,512]{2,1,0:T(8,128)}) %reduce-scatter.5.cloned.1.call-update) | async-done | bytes 32784 | tf_op jit(solution)/shard_map/reduce_scatter | solution.py:48
  239.2 12.9 %all_gather.10 = f32[4,16,512]{2,1,0:T(8,128)} all-gather(f32[1,16,512]{2,1,0:T(8,128)} %reduce-scatter.5.cloned.1.call-done), channel_id=1, replica_groups=mesh['row_0'=8,'row_1'=4,'col'=8] {'row_1'}, dimensions={0}, use_global_device_ids=true | all-gather | bytes 163840 | tf_op jit(solution)/shard_map/all_gather | solution.py:55
  252.2 1.3 fusion.5
  253.5 0.9 rev.3
  254.4 1.2 copy.29
  255.7 2.5 fusion.117
  258.2 10.1 %all-to-all-start.2 = ((f32[32,16,384]{2,1,0:T(8,128)}), f32[32,16,384]{2,1,0:T(8,128)S(1)}, u32[]{:S(2)}, u32[]{:S(2)}) async-start(f32[32,16,384]{2,1,0:T(8,128)} %fusion.117), calls=%async_computation.2 | async-start | bytes 1572864 | tf_op jit(solution)/shard_map/all_to_all | solution.py:78
  268.4 2.5 fusion
  272.5 0.9 fusion.116
  273.4 0.9 copy-done.9
  274.2 0.8 slice.179
  275.1 18.3 %all-to-all-done.2 = f32[32,16,384]{2,1,0:T(8,128)S(1)} async-done(((f32[32,16,384]{2,1,0:T(8,128)}), f32[32,16,384]{2,1,0:T(8,128)S(1)}, u32[]{:S(2)}, u32[]{:S(2)}) %all-to-all-start.2) | async-done | bytes 786464 | tf_op jit(solution)/shard_map/all_to_all | solution.py:78
  293.4 0.8 collective-permute-start
  294.2 3.3 all-gather.5.cloned.1.call-done
  297.5 3.4 %fusion.3 = f32[512,512]{1,0:T(8,128)S(1)} fusion(f32[512,512]{1,0:T(8,128)} %bitcast.131, f32[1024,1024]{1,0:T(8,128)} %copy-done), kind=kOutput, calls=%fused_computation.32 | convolution fusion | flops 1610612736 | bytes 3145728 | tf_op jit(solution)/shard_map/dot_general | solution.py:87
  300.9 4.7 %gather_fusion = f32[512]{0:T(512)S(1)} fusion(f32[512,512]{1,0:T(8,128)S(1)} %fusion.3, s32[512]{0:T(512)S(1)} %bitcast.112), kind=kCustom, calls=%fused_computation | custom fusion | bytes 8192 | tf_op jit(solution)/shard_map/jit(_diag)/jit(diagonal)/cond/branch_0_fun/gather | solution.py:93
  311.1 1.0 convolution_subtract_fusion.1
  312.5 1.5 convolution_subtract_fusion.5
  315.1 4.5 %gather_fusion.1 = f32[512]{0:T(512)S(1)} fusion(f32[512,512]{1,0:T(8,128)S(1)} %bitcast_add_fusion.2, s32[512]{0:T(512)S(1)} %bitcast.113), kind=kCustom, calls=%fused_computation.1 | custom fusion | bytes 8192 | tf_op jit(solution)/shard_map/jit(_diag)/jit(diagonal)/cond/branch_0_fun/gather | solution.py:93
  320.7 1.4 convolution_select_fusion.2
  322.5 1.7 slice_subtract_fusion
  324.6 0.8 copy.34
  (113 shorter events, 20.0 us)
Async XLA Ops:
  9.0 21.8 %all-to-all-start.1 = ((f32[8,288,1,128]{3,1,2,0:T(8,128)}), f32[8,288,1,128]{3,1,2,0:T(8,128)S(1)}, u32[]{:S(2)}, u32[]{:S(2)}) async-start(f32[8,288,1,128]{3,1,2,0:T(8,128)} %broadcast_in_dim.111), calls=%async_computation.1 | async-start | bytes 2359296 | tf_op jit(solution)/shard_map/all_to_all | solution.py:19
  13.5 18.2 %copy-start.15 = (f32[9,32,3,128]{3,1,2,0:T(8,128)S(1)}, f32[9,32,3,128]{3,1,2,0:T(8,128)}, u32[]{:S(2)}) copy-start(f32[9,32,3,128]{3,1,2,0:T(8,128)} %param.3) | copy-start | bytes 1327108
  13.5 104.2 %all-gather.3.cloned.1.call-start = ((), (), s32[]{:S(2)}) async-start(), calls=%async_computation.5 | async-start | bytes 5947392 | tf_op jit(solution)/shard_map/all_gather | solution.py:34
  32.2 1.2 copy-start.3
  33.4 20.8 %all-to-all-start = ((f32[8,288,1,128]{3,1,2,0:T(8,128)}), f32[8,288,1,128]{3,1,2,0:T(8,128)S(1)}, u32[]{:S(2)}, u32[]{:S(2)}) async-start(f32[8,288,1,128]{3,1,2,0:T(8,128)} %broadcast_in_dim.110), calls=%async_computation | async-start | bytes 2359296 | tf_op jit(solution)/shard_map/all_to_all | solution.py:19
  36.9 179.4 %reduce-scatter.3.cloned.1.call-start = ((), (), s32[]{:S(2)}) async-start(), calls=%async_computation.6 | async-start | bytes 1179648 | tf_op jit(solution)/shard_map/reduce_scatter | solution.py:48
  54.9 1.3 copy-start.1
  120.2 2.0 copy-start
  172.7 2.1 copy-start.6
  173.6 1.6 copy-start.14
  175.2 42.9 %copy-start.4 = (f32[288,128]{1,0:T(8,128)}, f32[288,128]{1,0:T(8,128)S(1)}, u32[]{:S(2)}) copy-start(f32[288,128]{1,0:T(8,128)S(1)} %fusion.65) | copy-start | bytes 442372
  177.2 39.4 %copy-start.11 = (f32[9,32,3,128]{3,1,2,0:T(8,128)S(1)}, f32[9,32,3,128]{3,1,2,0:T(8,128)}, u32[]{:S(2)}) copy-start(f32[9,32,3,128]{3,1,2,0:T(8,128)} %param.2) | copy-start | bytes 1327108
  178.9 60.3 %reduce-scatter.5.cloned.1.call-start = ((), (), s32[]{:S(2)}) async-start(), calls=%async_computation.7 | async-start | bytes 163840 | tf_op jit(solution)/shard_map/reduce_scatter | solution.py:48
  216.4 81.1 %all-gather.5.cloned.1.call-start = ((), (), s32[]{:S(2)}) async-start(), calls=%async_computation.8 | async-start | bytes 1179648 | tf_op jit(solution)/shard_map/all_gather | solution.py:55
  254.4 1.2 copy-start.13
  258.2 35.2 %all-to-all-start.2 = ((f32[32,16,384]{2,1,0:T(8,128)}), f32[32,16,384]{2,1,0:T(8,128)S(1)}, u32[]{:S(2)}, u32[]{:S(2)}) async-start(f32[32,16,384]{2,1,0:T(8,128)} %fusion.117), calls=%async_computation.2 | async-start | bytes 1572864 | tf_op jit(solution)/shard_map/all_to_all | solution.py:78
  268.4 4.1 %copy-start.5 = (f32[288,128]{1,0:T(8,128)S(1)}, f32[288,128]{1,0:T(8,128)}, u32[]{:S(2)}) copy-start(f32[288,128]{1,0:T(8,128)} %copy-done.4) | copy-start | bytes 442372
  270.9 0.8 copy-start.12
  273.4 0.9 copy-start.9
  293.4 29.1 %collective-permute-start = (f32[16,384]{1,0:T(8,128)S(1)}, f32[16,384]{1,0:T(8,128)S(1)}, u32[]{:S(2)}, u32[]{:S(2)}) collective-permute-start(f32[16,384]{1,0:T(8,128)S(1)} %reduce_sum.9), channel_id=1, source_target_pairs={{0,128},{8,136},{16,144},{24,152},{32,160},{40,168},{48,176},{56,1... | collective-permute-start | bytes 73736 | tf_op jit(solution)/shard_map/ppermute | solution.py:83
  305.7 1.0 copy-start.7
  320.1 2.0 copy-start.8
  320.1 2.0 copy-start.10
  322.2 1.9 copy-start.2
Sparse Core Ops, SparseCore 0:
  31.8 85.8 all-gather.2
  179.0 37.3 reduce-scatter.2
  218.9 20.3 reduce-scatter.4
  252.3 45.1 all-gather.4
where the time goes:
time: 333 us; the launch traced here: 332 us
  waiting for transfers between devices  169 us (51%)
  local copies, waits for them, and re-layouts  46.6 us (14%)
  other arithmetic  44.4 us (13%)
  matrix products  25.7 us (8%)
  starting transfers between devices  19.3 us (6%)
  between operations  13.9 us (4%)
  blocking collectives  12.9 us (4%)
    all_gather x1, waiting for transfers between devices, sent_together(): lax.all_gather(both, axis, axis=dim, tiled=True)  60.4 us
    reduce_scatter x2, waiting for transfers between devices, own_block(): blocks = lax.psum_scatter(blocks, axes[k], scatter_dimension=0, tiled=True)  55.3 us
    another operation x3, other arithmetic, local(): lax.linalg.triangular_solve(diag_block, adjoint_panels[:, first_row:botto...  40.2 us
    all_to_all x2, waiting for transfers between devices, sent_to_all(): lax.all_to_all(jnp.broadcast_to(array[None], (size, *array.shape)), axis,...  31.9 us
    all_to_all x1, waiting for transfers between devices, sent_and_summed(): lax.all_to_all(blocks, axis, split_axis=0, concat_axis=0, tiled=True)  18.3 us
    dot_general x8, matrix products, exact_dot(): jnp.dot(first, second, precision=lax.Precision.HIGHEST, preferred_element...  15.7 us
    all_gather x1, blocking collectives, all_blocks(): blocks = lax.all_gather(blocks, axes[k], axis=0, tiled=True)  12.9 us
    another operation x12, local copies, waits for them, and re-layouts  10.2 us
  transfers between devices with their start and end apart: 8, of which 7 were waited for; matrix products, arithmetic and copies ran while one was open for 14% of the time, Pallas kernels for 0%

commit v1 on v0

v1 whole, which is shorter than its diff:
```python
import jax
import jax.numpy as jnp
from jax import lax
from jax.experimental import pallas as pl
from jax.experimental.pallas import tpu as pltpu
from jax.sharding import Mesh
from jax.sharding import PartitionSpec as P

NB = 512
TILE = 128
ROW = ("z", "x")


def exact_dot(first, second, over=((1,), (0,))):
    return lax.dot_general(
        first, second, (over, ((), ())),
        precision=lax.Precision.HIGHEST, preferred_element_type=jnp.float32,
    )


def inverse_kernel(diag_ref, inv_ref):
    rows = lax.broadcasted_iota(jnp.int32, (TILE, TILE), 0)
    cols = lax.broadcasted_iota(jnp.int32, (TILE, TILE), 1)
    blocks = NB // TILE
    eye = rows == cols
    diag = [diag_ref[k, k * TILE : (k + 1) * TILE, :] for k in range(blocks)]
    inv = []
    for block in diag:
        on_diag = jnp.where(eye, block, 0.0)
        down = 1.0 / jnp.sum(on_diag, axis=1, keepdims=True)
        along = 1.0 / jnp.sum(on_diag, axis=0, keepdims=True)
        pair = (rows // 2 == cols // 2) & (rows > cols)
        inv.append(jnp.where(eye, down, 0.0) - jnp.where(pair, down * block * along, 0.0))
    size = 2
    while size < TILE:
        joined = (rows // (2 * size) == cols // (2 * size)) & (rows // size > cols // size)
        right = [exact_dot(jnp.where(joined, d, 0.0), i) for d, i in zip(diag, inv)]
        inv = [i - exact_dot(i, r) for i, r in zip(inv, right)]
        size *= 2
    inv_ref[...] = jnp.zeros((NB, NB), jnp.float32)
    for k in range(blocks):
        inv_ref[k * TILE : (k + 1) * TILE, k * TILE : (k + 1) * TILE] = inv[k]
    for k in (0, 2):
        lower = diag_ref[k, (k + 1) * TILE : (k + 2) * TILE, :]
        inv_ref[(k + 1) * TILE : (k + 2) * TILE, k * TILE : (k + 1) * TILE] = -exact_dot(
            inv[k + 1], exact_dot(lower, inv[k])
        )
    half = NB // 2
    corner = jnp.concatenate([diag_ref[0, half:, :], diag_ref[1, half:, :]], axis=1)
    inv_ref[half:, :half] = -exact_dot(inv_ref[half:, half:], exact_dot(corner, inv_ref[:half, :half]))


def inverse_of(diag_cols):
    return pl.pallas_call(
        inverse_kernel,
        out_shape=jax.ShapeDtypeStruct((NB, NB), jnp.float32),
        name="lower_inverse",
    )(diag_cols)


def panel_blocks(block):
    y, k = lax.axis_index("y"), lax.axis_index("k")
    near = lax.ppermute(block, "y", [(2, 1), (3, 0)])
    across = lax.ppermute(block, "y", [(2, 3), (3, 2)])
    far = lax.ppermute(block, "y", [(2, 0), (3, 1)])
    two = jnp.where(y == 2, block, jnp.where(y == 3, across, jnp.where(y == 1, near, far)))
    three = jnp.where(y == 3, block, jnp.where(y == 2, across, jnp.where(y == 0, near, far)))
    mine = jnp.stack([two, three])
    other = lax.ppermute(mine, "k", [(0, 1), (1, 0)])
    first, second = jnp.where(k == 0, mine, other), jnp.where(k == 0, other, mine)
    return jnp.stack([first[0], second[0], first[1], second[1]])


def to_all(block, axis):
    size = lax.axis_size(axis)
    return lax.all_to_all(
        jnp.broadcast_to(block[None], (size, *block.shape)), axis, 0, 0, tiled=True
    )


def side_by_side(blocks):
    return jnp.moveaxis(blocks, 0, 1).reshape(blocks.shape[1], -1)


def local(factor, adjoint):
    z, row = lax.axis_index("z"), lax.axis_index(ROW)
    col = lax.axis_index("y") * 2 + lax.axis_index("k")
    low = z >= 4
    owner = col >= 4
    f0, f1, f2 = (factor[:, :, e, :].reshape(288, TILE) for e in range(3))
    a0, a1, a2 = (adjoint[:, :, e, :].reshape(288, TILE) for e in range(3))
    own_rows = row * 32 + jnp.arange(32, dtype=jnp.int32)
    own_cols = col * TILE + jnp.arange(TILE, dtype=jnp.int32)
    a2_top = jnp.where(own_cols[None, :] > own_rows[:, None], 0.0, a2[:32])
    a2 = jnp.concatenate([a2_top, a2[32:]], 0)

    last = to_all(f2[:32], ROW)[16:].reshape(NB, TILE)
    left = jnp.concatenate([f0[:32], f1[:32]], 1)
    handed = lax.ppermute(left[16:], "z", [(i, i - 4) for i in range(4, 8)])
    sent = jnp.where(low, left[:16], handed)
    arrived = to_all(sent, ROW)
    left_rows = jnp.stack([arrived[16:], arrived[:16]], 1).reshape(NB, 2 * TILE)

    panels = panel_blocks(jnp.concatenate([a2, f2], 0))
    diag_cols = panel_blocks(last)
    inverse = inverse_of(diag_cols)

    adj_panel = side_by_side(panels[:, :288])
    fac_panel = side_by_side(panels[:, 288:])
    weights = adj_panel[32:]
    top = jnp.where(low, 1.0, 0.0)
    first = jnp.concatenate([fac_panel[:32] * top, weights], 0)
    second = jnp.concatenate([-adj_panel[:32] * top, fac_panel[32:]], 0)
    steps = jnp.arange(NB, dtype=jnp.int32)
    kept = steps[:, None] >= steps[None, :]
    over_rows = ((0,), (0,))
    middle = -jnp.where(
        kept, exact_dot(first, second, over_rows), exact_dot(second, first, over_rows)
    )
    eye_cols = (steps[:, None] == (own_cols - 512)[None, :]).astype(jnp.float32)
    right = jnp.concatenate([left_rows, jnp.where(owner, eye_cols, last)], 1)
    below = jnp.concatenate([f0[32:], f1[32:], jnp.where(owner, 0.0, f2[32:])], 1)
    solved = exact_dot(inverse, right)
    inner = exact_dot(weights, below, over_rows) + exact_dot(middle, solved)
    partial = exact_dot(inverse, inner, over_rows)
    halves = partial.reshape(16, 2, 16, 3 * TILE)
    parts = jnp.concatenate([halves[:, 1], halves[:, 0]], 0)
    share = lax.all_to_all(parts, ROW, 0, 0, tiled=True).sum(axis=0)
    partner = lax.ppermute(share, "z", [(i, i + 4) for i in range(4)])
    change = jnp.concatenate([share, partner], 0)

    update = exact_dot(weights, solved)
    tops = jnp.concatenate([a0[:32], a1[:32], a2_top], 1)
    gap = own_rows[:, None] - own_cols[None, :]
    halved = jnp.where(gap > 0, 1.0, jnp.where(gap == 0, 0.5, 0.0)) * change[:, 2 * TILE :]
    new_diag = jnp.where(owner, halved, tops[:, 2 * TILE :] - change[:, 2 * TILE :])
    new_top = jnp.concatenate([tops[:, : 2 * TILE] - change[:, : 2 * TILE], new_diag], 1)
    new_top = jnp.where(low, new_top, tops)
    new_below = jnp.concatenate(
        [
            a0[32:] - update[:, :TILE],
            a1[32:] - update[:, TILE : 2 * TILE],
            jnp.where(owner, update[:, 2 * TILE :], a2[32:] - update[:, 2 * TILE :]),
        ],
        1,
    )
    return jnp.concatenate([new_top, new_below], 0).reshape(9, 32, 3, TILE)


def solution(mesh):
    split = Mesh(mesh.devices.reshape(8, 4, 4, 2), ("z", "x", "y", "k"))
    placed = P(None, ROW, None, ("y", "k"))
    return jax.shard_map(
        local, mesh=split, in_specs=(placed, placed), out_specs=placed, check_vma=False
    )
```

time: 333 us -> 127 us (0.38)
  waiting for transfers between devices: 169 us -> 50.5 us
  local copies, waits for them, and re-layouts: 46.6 us -> 8.27 us
  other arithmetic: 44.4 us -> 8.91 us
  starting transfers between devices: 19.3 us -> 38.3 us
  between operations: 13.9 us -> 0.55 us
  blocking collectives: 12.9 us -> 0 us
  matrix products: 25.7 us -> 13 us
  Pallas kernels: 0 us -> 6.64 us
    all_gather x2 -> x0, waiting for transfers between devices: 63.6 us -> none  [the longest x1 60.4 us: sent_together(): lax.all_gather(both, axis, axis=dim, tiled=True)]
    reduce_scatter x2 -> x0, waiting for transfers between devices: 55.3 us -> none  [own_block(): blocks = lax.psum_scatter(blocks, axes[k], scatter_dimension=0, tiled=True)]
    another operation x5 -> x7, other arithmetic: 40.4 us -> 3.7 us  [the longest x4 1.74 us: panel_blocks(): mine = jnp.stack([two, three])]
    ppermute x1 -> x10, waiting for transfers between devices: 0.01 us -> 29.5 us  [the longest x2 17.6 us: panel_blocks(): near = lax.ppermute(block, 'y', [(2, 1), (3, 0)])]
    all_to_all x3, waiting for transfers between devices: 50.1 us -> 21 us  [the longest x1 21 us: local(): share = lax.all_to_all(parts, ROW, 0, 0, tiled=True).sum(axis=0)]
    another operation x18 -> x1, local copies, waits for them, and re-layouts: 13.7 us -> 0.04 us  [local(): left_rows = jnp.stack([arrived[16:], arrived[:16]], 1).reshape(NB, 2 * TILE)]
    all_gather x1 -> x0, blocking collectives: 12.9 us -> none  [all_blocks(): blocks = lax.all_gather(blocks, axes[k], axis=0, tiled=True)]
    ppermute x1 -> x10, starting transfers between devices: 0.81 us -> 11 us  [the longest x1 3.07 us: local(): partner = lax.ppermute(share, 'z', [(i, i + 4) for i in range(4)])]
  transfers between devices with their start and end apart: 8 -> 13, of which waited for: 7 -> 6; matrix products, arithmetic and copies ran while one was open for 14% -> 11% of each run, Pallas kernels for 0% -> 0%
where the time goes in v1:
time: 127 us; the launch traced here: 126 us
  waiting for transfers between devices  50.5 us (40%)
  starting transfers between devices  38.3 us (30%)
  matrix products  13 us (10%)
  other arithmetic  8.91 us (7%)
  local copies, waits for them, and re-layouts  8.27 us (7%)
  Pallas kernels  6.64 us (5%)
    all_to_all x1, waiting for transfers between devices, local(): share = lax.all_to_all(parts, ROW, 0, 0, tiled=True).sum(axis=0)  21 us
    ppermute x2, waiting for transfers between devices, panel_blocks(): near = lax.ppermute(block, 'y', [(2, 1), (3, 0)])  17.6 us
    all_to_all x2, starting transfers between devices, to_all(): lax.all_to_all(jnp.broadcast_to(block[None], (size, *block.shape)), axis,...  17.5 us
    dot_general x7, matrix products, exact_dot(): lax.dot_general(first, second, (over, ((), ())), precision=lax.Precision....  13 us
    ppermute x1, waiting for transfers between devices, local(): handed = lax.ppermute(left[16:], 'z', [(i, i - 4) for i in range(4, 8)])  10.1 us
    all_to_all x1, starting transfers between devices, local(): share = lax.all_to_all(parts, ROW, 0, 0, tiled=True).sum(axis=0)  9.77 us
    pallas_call x1, Pallas kernels, inverse_of(): pl.pallas_call(inverse_kernel, out_shape=jax.ShapeDtypeStruct((NB, NB), j...  6.64 us
    ppermute x1, starting transfers between devices, local(): partner = lax.ppermute(share, 'z', [(i, i + 4) for i in range(4)])  3.07 us
  transfers between devices with their start and end apart: 13, of which 6 were waited for; matrix products, arithmetic and copies ran while one was open for 11% of the time, Pallas kernels for 0%

profile of v1, /device:TPU:4, one launch (start us, length us, event | category | flops | bytes accessed | tf_op | source)
XLA Modules:
  0.0 126.1 jit_solution(9150578573526800953)
XLA Ops:
  0.0 1.8 %fusion.26 = (f32[8,32,1,128]{3,1,2,0:T(8,128)}, f32[8,32,1,128]{3,1,2,0:T(8,128)S(1)}, f32[8,32,1,128]{3,1,2,0:T(8,128)}) fusion(f32[9,32,3,128]{3,1,2,0:T(8,128)} %param.3), kind=kLoop, calls=%fused_computation.80 | loop fusion | bytes 786432 | tf_op jit(solution)/shard_map/slice | solution.py:141
  1.9 0.9 slice.192
  2.8 0.8 bitcast_select_fusion
  3.6 0.7 collective-permute-start.4
  4.3 1.3 %collective-permute-start.5 = (f32[576,128]{1,0:T(8,128)S(1)}, f32[576,128]{1,0:T(8,128)S(1)}, u32[]{:S(2)}, u32[]{:S(2)}) collective-permute-start(f32[576,128]{1,0:T(8,128)S(1)} %pad_maximum_fusion.12), channel_id=1, source_target_pairs={{4,2},{6,0},{5,3},{7,1},{12,10},{14,8},{13,11},{15,9},{20,18},{22,... | collective-permute-start | bytes 884744 | tf_op jit(solution)/shard_map/ppermute | solution.py:63
  5.6 1.3 %collective-permute-start.6 = (f32[576,128]{1,0:T(8,128)S(1)}, f32[576,128]{1,0:T(8,128)S(1)}, u32[]{:S(2)}, u32[]{:S(2)}) collective-permute-start(f32[576,128]{1,0:T(8,128)S(1)} %pad_maximum_fusion.12), channel_id=1, source_target_pairs={{4,0},{6,2},{5,1},{7,3},{12,8},{14,10},{13,9},{15,11},{20,16},{22,... | collective-permute-start | bytes 884744 | tf_op jit(solution)/shard_map/ppermute | solution.py:65
  6.9 0.9 broadcast_in_dim.24
  7.8 11.6 %all-to-all-start = ((f32[32,32,128]{2,1,0:T(8,128)}), f32[32,32,128]{2,1,0:T(8,128)}, u32[]{:S(2)}, u32[]{:S(2)}) async-start(f32[32,32,128]{2,1,0:T(8,128)} %broadcast_in_dim.24), calls=%async_computation | async-start | bytes 1048576 | tf_op jit(solution)/shard_map/all_to_all | solution.py:76
  19.5 4.1 %collective-permute-done.5 = f32[576,128]{1,0:T(8,128)S(1)} collective-permute-done((f32[576,128]{1,0:T(8,128)S(1)}, f32[576,128]{1,0:T(8,128)S(1)}, u32[]{:S(2)}, u32[]{:S(2)}) %collective-permute-start.5) | collective-permute-done | bytes 294944 | tf_op jit(solution)/shard_map/ppermute | solution.py:63
  23.7 0.1 collective-permute-start.7
  23.9 1.3 %collective-permute-start.8 = (f32[16,256]{1,0:T(8,128)S(1)}, f32[16,256]{1,0:T(8,128)S(1)}, u32[]{:S(2)}, u32[]{:S(2)}) collective-permute-start(f32[16,256]{1,0:T(8,128)S(1)} %pad_maximum_fusion.14), channel_id=1, source_target_pairs={{128,0},{160,32},{192,64},{224,96},{129,1},{161,33},{193,65},{225,... | collective-permute-start | bytes 49160 | tf_op jit(solution)/shard_map/ppermute | solution.py:99
  25.2 0.8 fusion.25
  25.9 0.5 broadcast_add_fusion
  26.4 10.1 %collective-permute-done.8 = f32[16,256]{1,0:T(8,128)S(1)} collective-permute-done((f32[16,256]{1,0:T(8,128)S(1)}, f32[16,256]{1,0:T(8,128)S(1)}, u32[]{:S(2)}, u32[]{:S(2)}) %collective-permute-start.8) | collective-permute-done | bytes 16416 | tf_op jit(solution)/shard_map/ppermute | solution.py:99
  37.0 0.2 copy.16
  37.2 0.2 copy.20
  37.4 0.1 copy.25
  37.6 0.1 copy.26
  37.7 0.9 broadcast_in_dim.44
  38.6 5.9 %all-to-all-start.1 = ((f32[32,16,256]{2,1,0:T(8,128)}), f32[32,16,256]{2,1,0:T(8,128)S(1)}, u32[]{:S(2)}, u32[]{:S(2)}) async-start(f32[32,16,256]{2,1,0:T(8,128)} %broadcast_in_dim.44), calls=%async_computation.1 | async-start | bytes 1048576 | tf_op jit(solution)/shard_map/all_to_all | solution.py:76
  44.5 2.1 %fusion.5 = f32[512,512]{1,0:T(8,128)S(1)} fusion(f32[256,512]{0,1:T(8,128)S(1)} %bitcast.72, f32[32,512]{0,1:T(8,128)S(1)} %bitcast.77, f32[256,512]{0,1:T(8,128)S(1)} %bitcast.68, f32[32,512]{0,1:T(8,128)S(1)} %bitcast.75), kind=kOutput, calls=%fused_computation.13 | convolution fusion | flops 906264576 | bytes 2228224 | tf_op jit(solution)/shard_map/dot_general | solution.py:15
  46.5 1.0 slice.229
  47.5 0.7 collective-permute-start
  48.2 1.3 %collective-permute-start.1 = (f32[512,128]{1,0:T(8,128)S(1)}, f32[512,128]{1,0:T(8,128)S(1)}, u32[]{:S(2)}, u32[]{:S(2)}) collective-permute-start(f32[512,128]{1,0:T(8,128)S(1)} %bitcast.85), channel_id=1, source_target_pairs={{4,2},{6,0},{5,3},{7,1},{12,10},{14,8},{13,11},{15,9},{20,18},{22,... | collective-permute-start | bytes 786440 | tf_op jit(solution)/shard_map/ppermute | solution.py:63
  49.5 1.3 %collective-permute-start.2 = (f32[512,128]{1,0:T(8,128)S(1)}, f32[512,128]{1,0:T(8,128)S(1)}, u32[]{:S(2)}, u32[]{:S(2)}) collective-permute-start(f32[512,128]{1,0:T(8,128)S(1)} %bitcast.86), channel_id=1, source_target_pairs={{4,0},{6,2},{5,1},{7,3},{12,8},{14,10},{13,9},{15,11},{20,16},{22,... | collective-permute-start | bytes 786440 | tf_op jit(solution)/shard_map/ppermute | solution.py:65
  50.8 2.1 %fusion = f32[512,512]{1,0:T(8,128)S(1)} fusion(f32[512,512]{1,0:T(8,128)S(1)} %fusion.5, f32[256,512]{0,1:T(8,128)S(1)} %bitcast.73, f32[32,512]{0,1:T(8,128)S(1)} %bitcast.78, f32[256,512]{0,1:T(8,128)S(1)} %bitcast.69, f32[32,512]{0,1:T(8,128)S(1)} %bitcast.76), kind=kOutput, calls=%fused_computation.1 | convolution fusion | flops 907051008 | bytes 3276800 | tf_op jit(solution)/shard_map/dot_general | solution.py:15
  52.9 13.5 %collective-permute-done.1 = f32[512,128]{1,0:T(8,128)S(1)} collective-permute-done((f32[512,128]{1,0:T(8,128)S(1)}, f32[512,128]{1,0:T(8,128)S(1)}, u32[]{:S(2)}, u32[]{:S(2)}) %collective-permute-start.1) | collective-permute-done | bytes 262176 | tf_op jit(solution)/shard_map/ppermute | solution.py:63
  66.4 0.8 select_bitcast_fusion.3
  67.2 0.8 pad_maximum_fusion.10
  68.0 1.0 fusion.6
  69.1 0.8 pad_maximum_fusion.11
  69.9 0.3 collective-permute-done.3
  70.3 1.1 broadcast_select_fusion.3
  71.5 1.0 pad_maximum_fusion.1.diag_ref
  72.5 6.6 %lower_inverse.1 = f32[512,512]{1,0:T(8,128)} custom-call(f32[4,512,128]{2,1,0:T(8,128)} %pad_maximum_fusion.1.diag_ref), custom_call_target="tpu_custom_call" | custom-call | tf_op jit(solution)/shard_map/lower_inverse/pallas_call | solution.py:54
  79.1 3.2 %fusion.1 = f32[512,384]{1,0:T(8,128)S(1)} fusion(f32[512,512]{1,0:T(8,128)} %lower_inverse.1, f32[512,128]{1,0:T(8,128)S(1)} %copy-done.1, f32[512,256]{1,0:T(8,128)} %bitcast.79), kind=kOutput, calls=%fused_computation.8 | convolution fusion | flops 1208156160 | bytes 2621440 | tf_op jit(solution)/shard_map/dot_general | solution.py:15
  82.3 1.8 %convolution_add_fusion = f32[512,384]{1,0:T(8,128)S(1)} fusion(f32[512,384]{1,0:T(8,128)S(1)} %fusion.6, f32[512,512]{1,0:T(8,128)S(1)} %fusion, f32[512,384]{1,0:T(8,128)S(1)} %fusion.1), kind=kOutput, calls=%fused_computation.2 | convolution fusion | flops 1208156160 | bytes 3407872 | tf_op jit(solution)/shard_map/dot_general | solution.py:15
  84.1 1.8 %fusion.27 = f32[512,384]{1,0:T(8,128)S(1)} fusion(f32[512,512]{1,0:T(8,128)S(1)} %copy-done, f32[512,384]{1,0:T(8,128)S(1)} %convolution_add_fusion), kind=kOutput, calls=%fused_computation.81 | convolution fusion | flops 1207959552 | bytes 2621440 | tf_op jit(solution)/shard_map/dot_general | solution.py:15
  86.1 0.9 pad_maximum_fusion.4
  87.0 9.8 %all-to-all-start.2 = ((f32[32,16,384]{2,1,0:T(8,128)}), f32[32,16,384]{2,1,0:T(8,128)S(1)}, u32[]{:S(2)}, u32[]{:S(2)}) async-start(f32[32,16,384]{2,1,0:T(8,128)} %pad_maximum_fusion.4), calls=%async_computation.2 | async-start | bytes 1572864 | tf_op jit(solution)/shard_map/all_to_all | solution.py:128
  96.8 0.7 slice_bitcast_fusion.10
  97.5 1.0 fusion.28
  98.6 21.0 %all-to-all-done.2 = f32[32,16,384]{2,1,0:T(8,128)S(1)} async-done(((f32[32,16,384]{2,1,0:T(8,128)}), f32[32,16,384]{2,1,0:T(8,128)S(1)}, u32[]{:S(2)}, u32[]{:S(2)}) %all-to-all-start.2) | async-done | bytes 786464 | tf_op jit(solution)/shard_map/all_to_all | solution.py:128
  119.6 3.1 %collective-permute-start.9 = (f32[16,384]{1,0:T(8,128)S(1)}, f32[16,384]{1,0:T(8,128)S(1)}, u32[]{:S(2)}, u32[]{:S(2)}) collective-permute-start(f32[16,384]{1,0:T(8,128)S(1)} %reduce_sum.9), channel_id=1, source_target_pairs={{0,128},{32,160},{64,192},{96,224},{1,129},{33,161},{65,193},{97,2... | collective-permute-start | bytes 73736 | tf_op jit(solution)/shard_map/ppermute | solution.py:129
  122.8 1.4 %collective-permute-done.9 = f32[16,384]{1,0:T(8,128)S(1)} collective-permute-done((f32[16,384]{1,0:T(8,128)S(1)}, f32[16,384]{1,0:T(8,128)S(1)}, u32[]{:S(2)}, u32[]{:S(2)}) %collective-permute-start.9) | collective-permute-done | bytes 24608 | tf_op jit(solution)/shard_map/ppermute | solution.py:129
  124.2 0.8 subtract_select_fusion.1
  125.1 0.2 reshape.55
  125.3 0.8 copy.24
  (58 shorter events, 0.9 us)
Async XLA Ops:
  0.0 6.9 %copy-start.2 = (f32[9,32,3,128]{3,1,2,0:T(8,128)S(1)}, f32[9,32,3,128]{3,1,2,0:T(8,128)}, u32[]{:S(2)}) copy-start(f32[9,32,3,128]{3,1,2,0:T(8,128)} %param.2) | copy-start | bytes 1327108
  0.0 3.6 %copy-start.8 = (s32[128]{0:T(128)}, s32[128]{0:T(128)S(1)}, u32[]{:S(2)}) copy-start(s32[128]{0:T(128)S(1)} %iota_add_fusion.1) | copy-start | bytes 1540
  0.0 3.6 %copy-start.10 = (s32[32]{0:T(128)}, s32[32]{0:T(128)S(1)}, u32[]{:S(2)}) copy-start(s32[32]{0:T(128)S(1)} %iota_add_fusion) | copy-start | bytes 388
  3.6 15.8 %collective-permute-start.4 = (f32[576,128]{1,0:T(8,128)S(1)}, f32[576,128]{1,0:T(8,128)S(1)}, u32[]{:S(2)}, u32[]{:S(2)}) collective-permute-start(f32[576,128]{1,0:T(8,128)S(1)} %pad_maximum_fusion.12), channel_id=1, source_target_pairs={{4,6},{6,4},{5,7},{7,5},{12,14},{14,12},{13,15},{15,13},{20,22},{2... | collective-permute-start | bytes 884744 | tf_op jit(solution)/shard_map/ppermute | solution.py:64
  4.3 19.3 %collective-permute-start.5 = (f32[576,128]{1,0:T(8,128)S(1)}, f32[576,128]{1,0:T(8,128)S(1)}, u32[]{:S(2)}, u32[]{:S(2)}) collective-permute-start(f32[576,128]{1,0:T(8,128)S(1)} %pad_maximum_fusion.12), channel_id=1, source_target_pairs={{4,2},{6,0},{5,3},{7,1},{12,10},{14,8},{13,11},{15,9},{20,18},{22,... | collective-permute-start | bytes 884744 | tf_op jit(solution)/shard_map/ppermute | solution.py:63
  5.6 18.0 %collective-permute-start.6 = (f32[576,128]{1,0:T(8,128)S(1)}, f32[576,128]{1,0:T(8,128)S(1)}, u32[]{:S(2)}, u32[]{:S(2)}) collective-permute-start(f32[576,128]{1,0:T(8,128)S(1)} %pad_maximum_fusion.12), channel_id=1, source_target_pairs={{4,0},{6,2},{5,1},{7,3},{12,8},{14,10},{13,9},{15,11},{20,16},{22,... | collective-permute-start | bytes 884744 | tf_op jit(solution)/shard_map/ppermute | solution.py:65
  7.8 29.9 %all-to-all-start = ((f32[32,32,128]{2,1,0:T(8,128)}), f32[32,32,128]{2,1,0:T(8,128)}, u32[]{:S(2)}, u32[]{:S(2)}) async-start(f32[32,32,128]{2,1,0:T(8,128)} %broadcast_in_dim.24), calls=%async_computation | async-start | bytes 1048576 | tf_op jit(solution)/shard_map/all_to_all | solution.py:76
  23.7 12.8 %collective-permute-start.7 = (f32[2,576,128]{2,1,0:T(8,128)S(1)}, f32[2,576,128]{2,1,0:T(8,128)S(1)}, u32[]{:S(2)}, u32[]{:S(2)}) collective-permute-start(f32[2,576,128]{2,1,0:T(8,128)S(1)} %pad_maximum_fusion.9), channel_id=1, source_target_pairs={{0,1},{1,0},{2,3},{3,2},{4,5},{5,4},{6,7},{7,6},{8,9},{9,8},{10,11... | collective-permute-start | bytes 1769480 | tf_op jit(solution)/shard_map/ppermute | solution.py:69
  23.9 12.7 %collective-permute-start.8 = (f32[16,256]{1,0:T(8,128)S(1)}, f32[16,256]{1,0:T(8,128)S(1)}, u32[]{:S(2)}, u32[]{:S(2)}) collective-permute-start(f32[16,256]{1,0:T(8,128)S(1)} %pad_maximum_fusion.14), channel_id=1, source_target_pairs={{128,0},{160,32},{192,64},{224,96},{129,1},{161,33},{193,65},{225,... | collective-permute-start | bytes 49160 | tf_op jit(solution)/shard_map/ppermute | solution.py:99
  38.6 30.4 %all-to-all-start.1 = ((f32[32,16,256]{2,1,0:T(8,128)}), f32[32,16,256]{2,1,0:T(8,128)S(1)}, u32[]{:S(2)}, u32[]{:S(2)}) async-start(f32[32,16,256]{2,1,0:T(8,128)} %broadcast_in_dim.44), calls=%async_computation.1 | async-start | bytes 1048576 | tf_op jit(solution)/shard_map/all_to_all | solution.py:76
  47.5 18.9 %copy-start.12 = (s32[128]{0:T(128)S(1)}, s32[128]{0:T(128)}, u32[]{:S(2)}) copy-start(s32[128]{0:T(128)} %broadcast_add_fusion) | copy-start | bytes 1540
  47.5 5.4 %collective-permute-start = (f32[512,128]{1,0:T(8,128)S(1)}, f32[512,128]{1,0:T(8,128)S(1)}, u32[]{:S(2)}, u32[]{:S(2)}) collective-permute-start(f32[512,128]{1,0:T(8,128)S(1)} %bitcast.84), channel_id=1, source_target_pairs={{4,6},{6,4},{5,7},{7,5},{12,14},{14,12},{13,15},{15,13},{20,22},{2... | collective-permute-start | bytes 786440 | tf_op jit(solution)/shard_map/ppermute | solution.py:64
  48.2 18.2 %collective-permute-start.1 = (f32[512,128]{1,0:T(8,128)S(1)}, f32[512,128]{1,0:T(8,128)S(1)}, u32[]{:S(2)}, u32[]{:S(2)}) collective-permute-start(f32[512,128]{1,0:T(8,128)S(1)} %bitcast.85), channel_id=1, source_target_pairs={{4,2},{6,0},{5,3},{7,1},{12,10},{14,8},{13,11},{15,9},{20,18},{22,... | collective-permute-start | bytes 786440 | tf_op jit(solution)/shard_map/ppermute | solution.py:63
  49.5 16.9 %collective-permute-start.2 = (f32[512,128]{1,0:T(8,128)S(1)}, f32[512,128]{1,0:T(8,128)S(1)}, u32[]{:S(2)}, u32[]{:S(2)}) collective-permute-start(f32[512,128]{1,0:T(8,128)S(1)} %bitcast.86), channel_id=1, source_target_pairs={{4,0},{6,2},{5,1},{7,3},{12,8},{14,10},{13,9},{15,11},{20,16},{22,... | collective-permute-start | bytes 786440 | tf_op jit(solution)/shard_map/ppermute | solution.py:65
  52.9 15.1 %copy-start.5 = (f32[8,32,1,128]{3,1,2,0:T(8,128)S(1)}, f32[8,32,1,128]{3,1,2,0:T(8,128)}, u32[]{:S(2)}) copy-start(f32[8,32,1,128]{3,1,2,0:T(8,128)} %get-tuple-element.29) | copy-start | bytes 393220
  52.9 15.1 %copy-start.6 = (f32[8,32,1,128]{3,1,2,0:T(8,128)S(1)}, f32[8,32,1,128]{3,1,2,0:T(8,128)}, u32[]{:S(2)}) copy-start(f32[8,32,1,128]{3,1,2,0:T(8,128)} %get-tuple-element.30) | copy-start | bytes 393220
  52.9 15.1 %copy-start.7 = (f32[8,32,1,128]{3,1,2,0:T(8,128)S(1)}, f32[8,32,1,128]{3,1,2,0:T(8,128)}, u32[]{:S(2)}) copy-start(f32[8,32,1,128]{3,1,2,0:T(8,128)} %get-tuple-element.31) | copy-start | bytes 393220
  68.0 2.3 %collective-permute-start.3 = (f32[2,512,128]{2,1,0:T(8,128)}, f32[2,512,128]{2,1,0:T(8,128)}, u32[]{:S(2)}, u32[]{:S(2)}) collective-permute-start(f32[2,512,128]{2,1,0:T(8,128)} %pad_maximum_fusion.10), channel_id=1, source_target_pairs={{0,1},{1,0},{2,3},{3,2},{4,5},{5,4},{6,7},{7,6},{8,9},{9,8},{10,11... | collective-permute-start | bytes 1572872 | tf_op jit(solution)/shard_map/ppermute | solution.py:69
  72.5 6.6 %copy-start.1 = (f32[512,128]{1,0:T(8,128)S(1)}, f32[512,128]{1,0:T(8,128)}, u32[]{:S(2)}) copy-start(f32[512,128]{1,0:T(8,128)} %get-tuple-element.41) | copy-start | bytes 786436
  82.3 1.8 %copy-start = (f32[512,512]{1,0:T(8,128)S(1)}, f32[512,512]{1,0:T(8,128)}, u32[]{:S(2)}) copy-start(f32[512,512]{1,0:T(8,128)} %lower_inverse.1) | copy-start | bytes 3145732
  87.0 32.6 %all-to-all-start.2 = ((f32[32,16,384]{2,1,0:T(8,128)}), f32[32,16,384]{2,1,0:T(8,128)S(1)}, u32[]{:S(2)}, u32[]{:S(2)}) async-start(f32[32,16,384]{2,1,0:T(8,128)} %pad_maximum_fusion.4), calls=%async_computation.2 | async-start | bytes 1572864 | tf_op jit(solution)/shard_map/all_to_all | solution.py:128
  97.5 25.2 %copy-start.3 = (f32[8,32,1,128]{3,1,2,0:T(8,128)S(1)}, f32[8,32,1,128]{3,1,2,0:T(8,128)}, u32[]{:S(2)}) copy-start(f32[8,32,1,128]{3,1,2,0:T(8,128)} %get-tuple-element.32) | copy-start | bytes 393220
  97.5 25.2 %copy-start.4 = (f32[8,32,1,128]{3,1,2,0:T(8,128)S(1)}, f32[8,32,1,128]{3,1,2,0:T(8,128)}, u32[]{:S(2)}) copy-start(f32[8,32,1,128]{3,1,2,0:T(8,128)} %get-tuple-element.34) | copy-start | bytes 393220
  98.6 25.6 %copy-start.9 = (s32[128]{0:T(128)S(1)}, s32[128]{0:T(128)}, u32[]{:S(2)}) copy-start(s32[128]{0:T(128)} %copy-done.8) | copy-start | bytes 1540
  98.6 25.6 %copy-start.11 = (s32[32]{0:T(128)S(1)}, s32[32]{0:T(128)}, u32[]{:S(2)}) copy-start(s32[32]{0:T(128)} %copy-done.10) | copy-start | bytes 388
  119.6 4.6 %collective-permute-start.9 = (f32[16,384]{1,0:T(8,128)S(1)}, f32[16,384]{1,0:T(8,128)S(1)}, u32[]{:S(2)}, u32[]{:S(2)}) collective-permute-start(f32[16,384]{1,0:T(8,128)S(1)} %reduce_sum.9), channel_id=1, source_target_pairs={{0,128},{32,160},{64,192},{96,224},{1,129},{33,161},{65,193},{97,2... | collective-permute-start | bytes 73736 | tf_op jit(solution)/shard_map/ppermute | solution.py:129

commit v2 on v1

v2 whole, which is shorter than its diff:
```python
import jax
import jax.numpy as jnp
from jax import lax
from jax.experimental import pallas as pl
from jax.experimental.pallas import tpu as pltpu
from jax.sharding import Mesh
from jax.sharding import PartitionSpec as P

NB = 512
TILE = 128
WIDE = 3 * TILE
ROW = ("zh", "zl", "x")


def exact_dot(first, second, over=((1,), (0,)), precision=lax.Precision.HIGHEST):
    return lax.dot_general(
        first, second, (over, ((), ())),
        precision=precision, preferred_element_type=jnp.float32,
    )


def close_dot(first, second, over=((1,), (0,))):
    return exact_dot(first, second, over, lax.Precision.HIGH)


def split(value):
    high = value.astype(jnp.bfloat16)
    return high, (value - high.astype(jnp.float32)).astype(jnp.bfloat16)


def split_dot(first, second, over=((1,), (0,))):
    def dot(a, b):
        return lax.dot_general(a, b, (over, ((), ())), preferred_element_type=jnp.float32)

    return dot(first[0], second[0]) + (dot(first[0], second[1]) + dot(first[1], second[0]))


def blocks_inverse(diag_ref, inv_ref):
    rows = lax.broadcasted_iota(jnp.int32, (TILE, TILE), 0)
    cols = lax.broadcasted_iota(jnp.int32, (TILE, TILE), 1)
    blocks = NB // TILE
    eye = rows == cols
    diag = [diag_ref[k, k * TILE : (k + 1) * TILE, :] for k in range(blocks)]
    inv = []
    for block in diag:
        on_diag = jnp.where(eye, block, 0.0)
        down = 1.0 / jnp.sum(on_diag, axis=1, keepdims=True)
        along = 1.0 / jnp.sum(on_diag, axis=0, keepdims=True)
        pair = (rows // 2 == cols // 2) & (rows > cols)
        inv.append(jnp.where(eye, down, 0.0) - jnp.where(pair, down * block * along, 0.0))
    size = 2
    while size < TILE:
        joined = (rows // (2 * size) == cols // (2 * size)) & (rows // size > cols // size)
        right = [exact_dot(jnp.where(joined, d, 0.0), i) for d, i in zip(diag, inv)]
        inv = [i - exact_dot(i, r) for i, r in zip(inv, right)]
        size *= 2
    inv_ref[...] = jnp.zeros((NB, NB), jnp.float32)
    for k in range(blocks):
        inv_ref[k * TILE : (k + 1) * TILE, k * TILE : (k + 1) * TILE] = inv[k]
    for k in (0, 2):
        lower = diag_ref[k, (k + 1) * TILE : (k + 2) * TILE, :]
        inv_ref[(k + 1) * TILE : (k + 2) * TILE, k * TILE : (k + 1) * TILE] = -exact_dot(
            inv[k + 1], exact_dot(lower, inv[k])
        )
    half = NB // 2
    corner = jnp.concatenate([diag_ref[0, half:, :], diag_ref[1, half:, :]], axis=1)
    inv_ref[half:, :half] = -exact_dot(inv_ref[half:, half:], exact_dot(corner, inv_ref[:half, :half]))


def solve_kernel(
    place, pack0, pack1, pack2, pack3, left0, left1, left2, left3, outer, middle,
    solved_ref, part0, part1, part2, part3, diag, inv, right, partial,
):
    x, owner, offset = (place[i] for i in range(3))
    rows = lax.broadcasted_iota(jnp.int32, (32, TILE), 0)
    cols = lax.broadcasted_iota(jnp.int32, (32, TILE), 1) + offset
    packs, lefts = (pack0, pack1, pack2, pack3), (left0, left1, left2, left3)
    for step in range(4):
        at = 0
        for block in range(4):
            for zl in range(block, 4):
                start = pl.multiple_of((zl * 4 + (x - step) % 4) * 32, 32)
                diag[block, pl.ds(start, 32), :] = packs[step][at : at + 32, :]
                at += 32
        for zl in range(4):
            start = pl.multiple_of((zl * 4 + (x - step) % 4) * 32, 32)
            line = lefts[step][zl * 32 : (zl + 1) * 32, :]
            eye = (rows + start == cols).astype(jnp.float32)
            right[pl.ds(start, 32), : 2 * TILE] = line[:, : 2 * TILE]
            right[pl.ds(start, 32), 2 * TILE :] = jnp.where(owner == 1, eye, line[:, 2 * TILE :])
    blocks_inverse(diag, inv)
    inverse = split(inv[...])
    solved = split_dot(inverse, split(right[...]))
    solved_ref[...] = solved
    inner = outer[...] + split_dot(split(middle[...]), split(solved))
    partial[...] = split_dot(inverse, split(inner), ((0,), (0,)))
    for step, part in enumerate((part0, part1, part2, part3)):
        for zl in range(4):
            start = pl.multiple_of((zl * 4 + (x + step) % 4) * 32, 32)
            part[zl * 32 : (zl + 1) * 32, :] = partial[pl.ds(start, 32), :]


def spread_kernel(part0, part1, part2, part3, out):
    total = (part0[...] + part1[...]) + (part2[...] + part3[...])
    for zl in range(4):
        out[zl] = jnp.zeros((32, WIDE), jnp.float32)
        out[4 + zl] = total[zl * 32 : (zl + 1) * 32, :]


def spread_sum(*parts):
    parts = [pltpu.with_memory_space_constraint(p, pltpu.VMEM) for p in parts]
    return pl.pallas_call(
        spread_kernel,
        out_shape=pltpu.VMEM((8, 32, WIDE), jnp.float32),
        in_specs=[pl.BlockSpec(memory_space=pltpu.VMEM)] * 4,
        out_specs=pl.BlockSpec(memory_space=pltpu.VMEM),
        compiler_params=pltpu.CompilerParams(vmem_limit_bytes=8 << 20),
        name="spread",
    )(*parts)


def solved_parts(place, *arrays):
    arrays = [pltpu.with_memory_space_constraint(a, pltpu.VMEM) for a in arrays]
    part = pltpu.VMEM((TILE, WIDE), jnp.float32)
    return pl.pallas_call(
        solve_kernel,
        out_shape=(pltpu.VMEM((NB, WIDE), jnp.float32),) + (part,) * 4,
        in_specs=[pl.BlockSpec(memory_space=pltpu.SMEM)]
        + [pl.BlockSpec(memory_space=pltpu.VMEM)] * len(arrays),
        out_specs=(pl.BlockSpec(memory_space=pltpu.VMEM),) * 5,
        scratch_shapes=[
            pltpu.VMEM((4, NB, TILE), jnp.float32),
            pltpu.VMEM((NB, NB), jnp.float32),
            pltpu.VMEM((NB, WIDE), jnp.float32),
            pltpu.VMEM((NB, WIDE), jnp.float32),
        ],
        compiler_params=pltpu.CompilerParams(vmem_limit_bytes=24 << 20),
        name="solve",
    )(place, *arrays)


def over_x(block):
    blocks = block if isinstance(block, tuple) else (block,) * 3
    return tuple(
        lax.ppermute(b, "x", [(i, (i + s) % 4) for i in range(4)])
        for s, b in zip((1, 2, 3), blocks)
    )


def over_y(block):
    near = lax.ppermute(block, "y", [(2, 1), (3, 0)])
    across = lax.ppermute(block, "y", [(2, 3), (3, 2)])
    far = lax.ppermute(block, "y", [(2, 0), (3, 1)])
    return near, across, far


def own_pair(block, near, across, far):
    inside = lax.axis_index("y") >= 2
    return jnp.where(inside, across, near), jnp.where(inside, block, far)


def swap(value):
    return lax.ppermute(value, "k", [(0, 1), (1, 0)])


def ordered(near, rest, other_near, other_rest):
    odd, k = lax.axis_index("y") % 2 == 1, lax.axis_index("k") == 1
    low, high = jnp.where(odd, near, rest), jnp.where(odd, rest, near)
    other_low = jnp.where(odd, other_near, other_rest)
    other_high = jnp.where(odd, other_rest, other_near)
    return (
        jnp.where(k, other_low, low), jnp.where(k, low, other_low),
        jnp.where(k, other_high, high), jnp.where(k, high, other_high),
    )


def panel_blocks(block, sent, earlier):
    sent = lax.optimization_barrier((*sent, earlier))[:3]
    near, rest = own_pair(block, *sent)
    return ordered(near, rest, swap(near), swap(rest))


def to_all(block, axis):
    size = lax.axis_size(axis)
    return lax.all_to_all(
        jnp.broadcast_to(block[None], (size, *block.shape)), axis, 0, 0, tiled=True
    )


def step(factor, adjoint):
    row, x = lax.axis_index(ROW), lax.axis_index("x")
    col = lax.axis_index("y") * 2 + lax.axis_index("k")
    low = lax.axis_index("zh") == 1
    owner = col >= 4
    f0, f1, f2 = (factor[:, :, e, :].reshape(288, TILE) for e in range(3))
    a0, a1, a2 = (adjoint[:, :, e, :].reshape(288, TILE) for e in range(3))
    own_rows = row * 32 + jnp.arange(32, dtype=jnp.int32)
    own_cols = col * TILE + jnp.arange(TILE, dtype=jnp.int32)
    a2_top = jnp.where(own_cols[None, :] > own_rows[:, None], 0.0, a2[:32])
    a2 = jnp.concatenate([a2_top, a2[32:]], 0)

    tops_l = jnp.concatenate([f0[:32], f1[:32], f2[:32]], 1)
    lines = to_all(tops_l, ("zh", "zl"))[4:].reshape(TILE, WIDE)
    sent = over_y(jnp.concatenate([a2, f2], 0))
    last = lines[:, 2 * TILE :]
    near, rest = own_pair(last, *over_y(last))
    lefts = (lines, *over_x(lines))
    quads = ordered(near, rest, swap(near), swap(rest))
    pack = jnp.concatenate([quads[c][32 * c :] for c in range(4)], 0)
    packs = (pack, *over_x(pack))
    panels = panel_blocks(jnp.concatenate([a2, f2], 0), sent, near)
    adj_panel = jnp.concatenate([p[:288] for p in panels], 1)
    fac_panel = jnp.concatenate([p[288:] for p in panels], 1)

    weights = adj_panel[32:]
    top = jnp.where(low, 1.0, 0.0)
    first = jnp.concatenate([fac_panel[:32] * top, weights], 0)
    second = jnp.concatenate([-adj_panel[:32] * top, fac_panel[32:]], 0)
    steps = jnp.arange(NB, dtype=jnp.int32)
    kept = steps[:, None] >= steps[None, :]
    over_rows = ((0,), (0,))
    middle = -jnp.where(
        kept, close_dot(first, second, over_rows), close_dot(second, first, over_rows)
    )
    below = jnp.concatenate([f0[32:], f1[32:], jnp.where(owner, 0.0, f2[32:])], 1)
    outer = close_dot(weights, below, over_rows)
    place = jnp.stack(
        [x, owner.astype(jnp.int32), col * TILE - 512]
    ).astype(jnp.int32)
    solved, *parts = solved_parts(place, *packs, *lefts, outer, middle)
    moved = over_x(tuple(parts[1:]))
    spread = spread_sum(parts[0], *moved)
    change = lax.all_to_all(spread, ("zh", "zl"), 0, 0, tiled=True).sum(axis=0)

    update = close_dot(weights, solved)
    tops = jnp.concatenate([a0[:32], a1[:32], a2_top], 1)
    gap = own_rows[:, None] - own_cols[None, :]
    halved = jnp.where(gap > 0, 1.0, jnp.where(gap == 0, 0.5, 0.0)) * change[:, 2 * TILE :]
    new_diag = jnp.where(owner, halved, tops[:, 2 * TILE :] - change[:, 2 * TILE :])
    new_top = jnp.concatenate([tops[:, : 2 * TILE] - change[:, : 2 * TILE], new_diag], 1)
    new_top = jnp.where(low, new_top, tops)
    new_below = jnp.concatenate(
        [
            a0[32:] - update[:, :TILE],
            a1[32:] - update[:, TILE : 2 * TILE],
            jnp.where(owner, update[:, 2 * TILE :], a2[32:] - update[:, 2 * TILE :]),
        ],
        1,
    )
    return jnp.concatenate([new_top, new_below], 0).reshape(9, 32, 3, TILE)


def solution(mesh):
    split_mesh = Mesh(
        mesh.devices.reshape(2, 4, 4, 4, 2), ("zh", "zl", "x", "y", "k")
    )
    placed = P(None, ROW, None, ("y", "k"))
    return jax.shard_map(
        step, mesh=split_mesh, in_specs=(placed, placed), out_specs=placed, check_vma=False
    )
```

time: 127 us -> 101 us (0.80)
  the two profiles are of different devices: /device:TPU:4 before, /device:TPU:7 now
where the time goes in v2:
time: 101 us
  waiting for transfers between devices  51.6 us (51%)
  starting transfers between devices  33 us (33%)
  Pallas kernels  8.41 us (8%)
  matrix products  3.3 us (3%)
  local copies, waits for them, and re-layouts  2.73 us (3%)
  other arithmetic  1.43 us (1%)
    ppermute x9, waiting for transfers between devices, over_x(): lax.ppermute(b, 'x', [(i, (i + s) % 4) for i in range(4)])  17.8 us
    all_to_all x1, waiting for transfers between devices, step(): change = lax.all_to_all(spread, ('zh', 'zl'), 0, 0, tiled=True).sum(axis=0)  14.4 us
    all_to_all x1, waiting for transfers between devices, to_all(): lax.all_to_all(jnp.broadcast_to(block[None], (size, *block.shape)), axis,...  10.1 us
    all_to_all x1, starting transfers between devices, to_all(): lax.all_to_all(jnp.broadcast_to(block[None], (size, *block.shape)), axis,...  8.32 us
    pallas_call x1, Pallas kernels, solved_parts(): pl.pallas_call(solve_kernel, out_shape=(pltpu.VMEM((NB, WIDE), jnp.float3...  7.62 us
    ppermute x9, starting transfers between devices, over_x(): lax.ppermute(b, 'x', [(i, (i + s) % 4) for i in range(4)])  7.28 us
    all_to_all x1, starting transfers between devices, step(): change = lax.all_to_all(spread, ('zh', 'zl'), 0, 0, tiled=True).sum(axis=0)  6.65 us
    ppermute x2, waiting for transfers between devices, over_y(): near = lax.ppermute(block, 'y', [(2, 1), (3, 0)])  5.69 us
  transfers between devices with their start and end apart: 21, of which 11 were waited for; matrix products, arithmetic and copies ran while one was open for 5% of the time, Pallas kernels for 0%

profile of v2, /device:TPU:7, one launch (start us, length us, event | category | flops | bytes accessed | tf_op | source)
XLA Modules:
  0.0 100.9 jit_solution(2886449520540334024)
XLA Ops:
  0.0 0.8 slice_bitcast_fusion.2
  0.8 0.8 broadcast_in_dim.30
  1.5 8.3 %all-to-all-start = ((f32[8,32,384]{2,1,0:T(8,128)}), f32[8,32,384]{2,1,0:T(8,128)S(1)}, u32[]{:S(2)}, u32[]{:S(2)}) async-start(f32[8,32,384]{2,1,0:T(8,128)} %broadcast_in_dim.30), calls=%async_computation | async-start | bytes 786432 | tf_op jit(solution)/shard_map/all_to_all | solution.py:185
  9.9 0.1 bitcast_select_fusion
  10.0 0.7 pad_maximum_fusion.4
  10.8 1.3 %collective-permute-start.11 = (f32[576,128]{1,0:T(8,128)}, f32[576,128]{1,0:T(8,128)S(1)}, u32[]{:S(2)}, u32[]{:S(2)}) collective-permute-start(f32[576,128]{1,0:T(8,128)} %pad_maximum_fusion.4), channel_id=1, source_target_pairs={{4,2},{6,0},{5,3},{7,1},{12,10},{14,8},{13,11},{15,9},{20,18},{22,... | collective-permute-start | bytes 884744 | tf_op jit(solution)/shard_map/ppermute | solution.py:151
  12.1 0.7 collective-permute-start.12
  12.7 1.3 %collective-permute-start.13 = (f32[576,128]{1,0:T(8,128)}, f32[576,128]{1,0:T(8,128)S(1)}, u32[]{:S(2)}, u32[]{:S(2)}) collective-permute-start(f32[576,128]{1,0:T(8,128)} %pad_maximum_fusion.4), channel_id=1, source_target_pairs={{4,0},{6,2},{5,1},{7,3},{12,8},{14,10},{13,9},{15,11},{20,16},{22,... | collective-permute-start | bytes 884744 | tf_op jit(solution)/shard_map/ppermute | solution.py:153
  14.1 10.1 %all-to-all-done = f32[8,32,384]{2,1,0:T(8,128)S(1)} async-done(((f32[8,32,384]{2,1,0:T(8,128)}), f32[8,32,384]{2,1,0:T(8,128)S(1)}, u32[]{:S(2)}, u32[]{:S(2)}) %all-to-all-start) | async-done | bytes 393248 | tf_op jit(solution)/shard_map/all_to_all | solution.py:185
  24.2 0.7 collective-permute-start
  24.9 1.3 %collective-permute-start.1 = (f32[128,128]{1,0:T(8,128)S(1)}, f32[128,128]{1,0:T(8,128)S(1)}, u32[]{:S(2)}, u32[]{:S(2)}) collective-permute-start(f32[128,128]{1,0:T(8,128)S(1)} %slice.207), channel_id=1, source_target_pairs={{4,2},{6,0},{5,3},{7,1},{12,10},{14,8},{13,11},{15,9},{20,18},{22,... | collective-permute-start | bytes 196616 | tf_op jit(solution)/shard_map/ppermute | solution.py:151
  26.2 1.3 %collective-permute-start.3 = (f32[128,128]{1,0:T(8,128)S(1)}, f32[128,128]{1,0:T(8,128)S(1)}, u32[]{:S(2)}, u32[]{:S(2)}) collective-permute-start(f32[128,128]{1,0:T(8,128)S(1)} %slice.207), channel_id=1, source_target_pairs={{4,0},{6,2},{5,1},{7,3},{12,8},{14,10},{13,9},{15,11},{20,16},{22,... | collective-permute-start | bytes 196616 | tf_op jit(solution)/shard_map/ppermute | solution.py:153
  27.5 0.1 pad_add_fusion.place
  27.6 5.7 %collective-permute-done.1 = f32[128,128]{1,0:T(8,128)S(1)} collective-permute-done((f32[128,128]{1,0:T(8,128)S(1)}, f32[128,128]{1,0:T(8,128)S(1)}, u32[]{:S(2)}, u32[]{:S(2)}) %collective-permute-start.1) | collective-permute-done | bytes 65568 | tf_op jit(solution)/shard_map/ppermute | solution.py:151
  33.3 0.5 collective-permute-start.10
  33.8 1.9 %collective-permute-done.3 = f32[128,128]{1,0:T(8,128)S(1)} collective-permute-done((f32[128,128]{1,0:T(8,128)S(1)}, f32[128,128]{1,0:T(8,128)S(1)}, u32[]{:S(2)}, u32[]{:S(2)}) %collective-permute-start.3) | collective-permute-done | bytes 65568 | tf_op jit(solution)/shard_map/ppermute | solution.py:153
  35.7 0.2 collective-permute-start.8
  36.0 2.2 %collective-permute-start.9 = (f32[128,384]{1,0:T(8,128)S(1)}, f32[128,384]{1,0:T(8,128)S(1)}, u32[]{:S(2)}, u32[]{:S(2)}) collective-permute-start(f32[128,384]{1,0:T(8,128)S(1)} %bitcast.33), channel_id=1, source_target_pairs={{0,16},{8,24},{16,0},{24,8},{1,17},{9,25},{17,1},{25,9},{2,18},{10... | collective-permute-start | bytes 589832 | tf_op jit(solution)/shard_map/ppermute | solution.py:145
  38.2 3.7 %collective-permute-start.2 = (f32[128,128]{1,0:T(8,128)S(1)}, f32[128,128]{1,0:T(8,128)S(1)}, u32[]{:S(2)}, u32[]{:S(2)}) collective-permute-start(f32[128,128]{1,0:T(8,128)S(1)} %get-tuple-element.25), channel_id=1, source_target_pairs={{0,1},{1,0},{2,3},{3,2},{4,5},{5,4},{6,7},{7,6},{8,9},{9,8},{10,11... | collective-permute-start | bytes 196616 | tf_op jit(solution)/shard_map/ppermute | solution.py:163
  41.8 0.1 collective-permute-start.4
  42.0 0.7 collective-permute-done.2
  42.7 0.4 collective-permute-start.15
  43.1 0.2 collective-permute-start.14
  43.3 1.0 collective-permute-done.15
  44.3 1.5 %collective-permute-start.5 = (f32[320,128]{1,0:T(8,128)S(1)}, f32[320,128]{1,0:T(8,128)S(1)}, u32[]{:S(2)}, u32[]{:S(2)}) collective-permute-start(f32[320,128]{1,0:T(8,128)S(1)} %pad_maximum_fusion.5.pack0), channel_id=1, source_target_pairs={{0,8},{8,16},{16,24},{24,0},{1,9},{9,17},{17,25},{25,1},{2,10},{10... | collective-permute-start | bytes 491528 | tf_op jit(solution)/shard_map/ppermute | solution.py:145
  45.9 0.1 broadcast_select_fusion.9
  46.0 0.1 fusion.22
  46.2 1.1 %fusion.2 = f32[512,512]{1,0:T(8,128)S(1)} fusion(f32[256,512]{1,0:T(8,128)S(1)} %slice.218, f32[32,512]{1,0:T(8,128)S(1)} %maximum_multiply_fusion, f32[288,128]{1,0:T(8,128)S(1)} %get-tuple-element.57, f32[288,128]{1,0:T(8,128)S(1)} %get-tuple-element.49, f32[288,128]{1,0:T(8,128)S(1)} %get-tuple-element.55, f32[288,128]{1,0:T(8,128)S(1)} %get-tuple-element.45, ...), kind=kOutput, calls=%fused_computation.10 | convolution fusion | flops 454459392 | bytes 2293760 | tf_op jit(solution)/shard_map/dot_general | solution.py:16
  47.2 1.0 %fusion.middle = f32[512,512]{1,0:T(8,128)S(1)} fusion(f32[512,512]{1,0:T(8,128)S(1)} %fusion.2, f32[256,512]{1,0:T(8,128)S(1)} %slice.218, f32[32,512]{1,0:T(8,128)S(1)} %maximum_multiply_fusion, f32[288,128]{1,0:T(8,128)S(1)} %get-tuple-element.57, f32[288,128]{1,0:T(8,128)S(1)} %get-tuple-element.49, f32[288,128]{1,0:T(8,128)S(1)} %get-tuple-element.55, ...), kind=kOutput, calls=%fused_computation.1 | convolution fusion | flops 455245824 | bytes 3342336 | tf_op jit(solution)/shard_map/dot_general | solution.py:16
  48.3 1.2 %collective-permute-start.7 = (f32[320,128]{1,0:T(8,128)S(1)}, f32[320,128]{1,0:T(8,128)S(1)}, u32[]{:S(2)}, u32[]{:S(2)}) collective-permute-start(f32[320,128]{1,0:T(8,128)S(1)} %pad_maximum_fusion.5.pack0), channel_id=1, source_target_pairs={{0,24},{8,0},{16,8},{24,16},{1,25},{9,1},{17,9},{25,17},{2,26},{10... | collective-permute-start | bytes 491528 | tf_op jit(solution)/shard_map/ppermute | solution.py:145
  49.6 0.6 fusion.3.outer
  50.2 2.3 %collective-permute-done.6.pack2 = f32[320,128]{1,0:T(8,128)S(1)} collective-permute-done((f32[320,128]{1,0:T(8,128)S(1)}, f32[320,128]{1,0:T(8,128)S(1)}, u32[]{:S(2)}, u32[]{:S(2)}) %collective-permute-start.6) | collective-permute-done | bytes 163872 | tf_op jit(solution)/shard_map/ppermute | solution.py:145
  52.5 4.4 %collective-permute-done.7.pack3 = f32[320,128]{1,0:T(8,128)S(1)} collective-permute-done((f32[320,128]{1,0:T(8,128)S(1)}, f32[320,128]{1,0:T(8,128)S(1)}, u32[]{:S(2)}, u32[]{:S(2)}) %collective-permute-start.7) | collective-permute-done | bytes 163872 | tf_op jit(solution)/shard_map/ppermute | solution.py:145
  56.9 7.6 %solve.1 = (f32[512,384]{1,0:T(8,128)S(1)}, f32[128,384]{1,0:T(8,128)S(1)}, f32[128,384]{1,0:T(8,128)S(1)}, f32[128,384]{1,0:T(8,128)S(1)}, f32[128,384]{1,0:T(8,128)S(1)}) custom-call(s32[3]{0:T(128)S(1)} %pad_add_fusion.place, f32[320,128]{1,0:T(8,128)S(1)} %pad_maximum_fusion.5.pack0, f32[320,128]{1,0:T(8,128)S(1)} %collective-permute-done.5.pack1, ...), custom_call_target="tpu_custom_call" | custom-call | tf_op jit(solution)/shard_map/solve/pallas_call | solution.py:125
  64.5 0.1 collective-permute-start.16
  64.6 0.1 collective-permute-start.17
  64.7 1.4 %collective-permute-start.18 = (f32[128,384]{1,0:T(8,128)S(1)}, f32[128,384]{1,0:T(8,128)S(1)}, u32[]{:S(2)}, u32[]{:S(2)}) collective-permute-start(f32[128,384]{1,0:T(8,128)S(1)} %get-tuple-element.19), channel_id=1, source_target_pairs={{0,24},{8,0},{16,8},{24,16},{1,25},{9,1},{17,9},{25,17},{2,26},{10... | collective-permute-start | bytes 589832 | tf_op jit(solution)/shard_map/ppermute | solution.py:145
  66.0 4.4 %collective-permute-done.16.part1 = f32[128,384]{1,0:T(8,128)S(1)} collective-permute-done((f32[128,384]{1,0:T(8,128)S(1)}, f32[128,384]{1,0:T(8,128)S(1)}, u32[]{:S(2)}, u32[]{:S(2)}) %collective-permute-start.16) | collective-permute-done | bytes 196640 | tf_op jit(solution)/shard_map/ppermute | solution.py:145
  70.4 1.2 %collective-permute-done.17.part2 = f32[128,384]{1,0:T(8,128)S(1)} collective-permute-done((f32[128,384]{1,0:T(8,128)S(1)}, f32[128,384]{1,0:T(8,128)S(1)}, u32[]{:S(2)}, u32[]{:S(2)}) %collective-permute-start.17) | collective-permute-done | bytes 196640 | tf_op jit(solution)/shard_map/ppermute | solution.py:145
  71.6 5.6 %collective-permute-done.18.part3 = f32[128,384]{1,0:T(8,128)S(1)} collective-permute-done((f32[128,384]{1,0:T(8,128)S(1)}, f32[128,384]{1,0:T(8,128)S(1)}, u32[]{:S(2)}, u32[]{:S(2)}) %collective-permute-start.18) | collective-permute-done | bytes 196640 | tf_op jit(solution)/shard_map/ppermute | solution.py:145
  77.2 0.8 spread.1
  78.0 6.7 %all-to-all-start.1 = ((f32[8,32,384]{2,1,0:T(8,128)}), f32[8,32,384]{2,1,0:T(8,128)S(1)}, u32[]{:S(2)}, u32[]{:S(2)}) async-start(f32[8,32,384]{2,1,0:T(8,128)} %spread.1), calls=%async_computation.1 | async-start | bytes 786432 | tf_op jit(solution)/shard_map/all_to_all | solution.py:233
  84.7 0.6 fusion.17
  85.3 0.1 slice_subtract_fusion.1
  85.3 14.4 %all-to-all-done.1 = f32[8,32,384]{2,1,0:T(8,128)S(1)} async-done(((f32[8,32,384]{2,1,0:T(8,128)}), f32[8,32,384]{2,1,0:T(8,128)S(1)}, u32[]{:S(2)}, u32[]{:S(2)}) %all-to-all-start.1) | async-done | bytes 393248 | tf_op jit(solution)/shard_map/all_to_all | solution.py:233
  99.7 0.1 subtract_select_fusion.1
  99.9 0.2 reshape.31
  100.1 0.8 copy.4
  (41 shorter events, 0.5 us)
Async XLA Ops:
  1.5 8.3 %copy-start = (f32[9,32,3,128]{3,1,2,0:T(8,128)S(1)}, f32[9,32,3,128]{3,1,2,0:T(8,128)}, u32[]{:S(2)}) copy-start(f32[9,32,3,128]{3,1,2,0:T(8,128)} %param.2) | copy-start | bytes 1327108
  1.5 8.4 %copy-start.1 = (f32[9,32,3,128]{3,1,2,0:T(8,128)S(1)}, f32[9,32,3,128]{3,1,2,0:T(8,128)}, u32[]{:S(2)}) copy-start(f32[9,32,3,128]{3,1,2,0:T(8,128)} %param.3) | copy-start | bytes 1327108
  1.5 22.6 %all-to-all-start = ((f32[8,32,384]{2,1,0:T(8,128)}), f32[8,32,384]{2,1,0:T(8,128)S(1)}, u32[]{:S(2)}, u32[]{:S(2)}) async-start(f32[8,32,384]{2,1,0:T(8,128)} %broadcast_in_dim.30), calls=%async_computation | async-start | bytes 786432 | tf_op jit(solution)/shard_map/all_to_all | solution.py:185
  10.8 25.2 %collective-permute-start.11 = (f32[576,128]{1,0:T(8,128)}, f32[576,128]{1,0:T(8,128)S(1)}, u32[]{:S(2)}, u32[]{:S(2)}) collective-permute-start(f32[576,128]{1,0:T(8,128)} %pad_maximum_fusion.4), channel_id=1, source_target_pairs={{4,2},{6,0},{5,3},{7,1},{12,10},{14,8},{13,11},{15,9},{20,18},{22,... | collective-permute-start | bytes 884744 | tf_op jit(solution)/shard_map/ppermute | solution.py:151
  12.1 26.1 %collective-permute-start.12 = (f32[576,128]{1,0:T(8,128)}, f32[576,128]{1,0:T(8,128)S(1)}, u32[]{:S(2)}, u32[]{:S(2)}) collective-permute-start(f32[576,128]{1,0:T(8,128)} %pad_maximum_fusion.4), channel_id=1, source_target_pairs={{4,6},{6,4},{5,7},{7,5},{12,14},{14,12},{13,15},{15,13},{20,22},{2... | collective-permute-start | bytes 884744 | tf_op jit(solution)/shard_map/ppermute | solution.py:152
  12.7 29.1 %collective-permute-start.13 = (f32[576,128]{1,0:T(8,128)}, f32[576,128]{1,0:T(8,128)S(1)}, u32[]{:S(2)}, u32[]{:S(2)}) collective-permute-start(f32[576,128]{1,0:T(8,128)} %pad_maximum_fusion.4), channel_id=1, source_target_pairs={{4,0},{6,2},{5,1},{7,3},{12,8},{14,10},{13,9},{15,11},{20,16},{22,... | collective-permute-start | bytes 884744 | tf_op jit(solution)/shard_map/ppermute | solution.py:153
  24.2 2.0 %collective-permute-start = (f32[128,128]{1,0:T(8,128)S(1)}, f32[128,128]{1,0:T(8,128)S(1)}, u32[]{:S(2)}, u32[]{:S(2)}) collective-permute-start(f32[128,128]{1,0:T(8,128)S(1)} %slice.207), channel_id=1, source_target_pairs={{4,6},{6,4},{5,7},{7,5},{12,14},{14,12},{13,15},{15,13},{20,22},{2... | collective-permute-start | bytes 196616 | tf_op jit(solution)/shard_map/ppermute | solution.py:152
  24.9 8.4 %collective-permute-start.1 = (f32[128,128]{1,0:T(8,128)S(1)}, f32[128,128]{1,0:T(8,128)S(1)}, u32[]{:S(2)}, u32[]{:S(2)}) collective-permute-start(f32[128,128]{1,0:T(8,128)S(1)} %slice.207), channel_id=1, source_target_pairs={{4,2},{6,0},{5,3},{7,1},{12,10},{14,8},{13,11},{15,9},{20,18},{22,... | collective-permute-start | bytes 196616 | tf_op jit(solution)/shard_map/ppermute | solution.py:151
  26.2 9.5 %collective-permute-start.3 = (f32[128,128]{1,0:T(8,128)S(1)}, f32[128,128]{1,0:T(8,128)S(1)}, u32[]{:S(2)}, u32[]{:S(2)}) collective-permute-start(f32[128,128]{1,0:T(8,128)S(1)} %slice.207), channel_id=1, source_target_pairs={{4,0},{6,2},{5,1},{7,3},{12,8},{14,10},{13,9},{15,11},{20,16},{22,... | collective-permute-start | bytes 196616 | tf_op jit(solution)/shard_map/ppermute | solution.py:153
  33.3 15.0 %collective-permute-start.10 = (f32[128,384]{1,0:T(8,128)S(1)}, f32[128,384]{1,0:T(8,128)S(1)}, u32[]{:S(2)}, u32[]{:S(2)}) collective-permute-start(f32[128,384]{1,0:T(8,128)S(1)} %bitcast.30), channel_id=1, source_target_pairs={{0,24},{8,0},{16,8},{24,16},{1,25},{9,1},{17,9},{25,17},{2,26},{10... | collective-permute-start | bytes 589832 | tf_op jit(solution)/shard_map/ppermute | solution.py:145
  35.7 14.5 %collective-permute-start.8 = (f32[128,384]{1,0:T(8,128)S(1)}, f32[128,384]{1,0:T(8,128)S(1)}, u32[]{:S(2)}, u32[]{:S(2)}) collective-permute-start(f32[128,384]{1,0:T(8,128)S(1)} %bitcast.31), channel_id=1, source_target_pairs={{0,8},{8,16},{16,24},{24,0},{1,9},{9,17},{17,25},{25,1},{2,10},{10... | collective-permute-start | bytes 589832 | tf_op jit(solution)/shard_map/ppermute | solution.py:145
  36.0 14.2 %collective-permute-start.9 = (f32[128,384]{1,0:T(8,128)S(1)}, f32[128,384]{1,0:T(8,128)S(1)}, u32[]{:S(2)}, u32[]{:S(2)}) collective-permute-start(f32[128,384]{1,0:T(8,128)S(1)} %bitcast.33), channel_id=1, source_target_pairs={{0,16},{8,24},{16,0},{24,8},{1,17},{9,25},{17,1},{25,9},{2,18},{10... | collective-permute-start | bytes 589832 | tf_op jit(solution)/shard_map/ppermute | solution.py:145
  38.2 4.6 %collective-permute-start.2 = (f32[128,128]{1,0:T(8,128)S(1)}, f32[128,128]{1,0:T(8,128)S(1)}, u32[]{:S(2)}, u32[]{:S(2)}) collective-permute-start(f32[128,128]{1,0:T(8,128)S(1)} %get-tuple-element.25), channel_id=1, source_target_pairs={{0,1},{1,0},{2,3},{3,2},{4,5},{5,4},{6,7},{7,6},{8,9},{9,8},{10,11... | collective-permute-start | bytes 196616 | tf_op jit(solution)/shard_map/ppermute | solution.py:163
  41.8 1.3 %collective-permute-start.4 = (f32[128,128]{1,0:T(8,128)S(1)}, f32[128,128]{1,0:T(8,128)S(1)}, u32[]{:S(2)}, u32[]{:S(2)}) collective-permute-start(f32[128,128]{1,0:T(8,128)S(1)} %get-tuple-element.26), channel_id=1, source_target_pairs={{0,1},{1,0},{2,3},{3,2},{4,5},{5,4},{6,7},{7,6},{8,9},{9,8},{10,11... | collective-permute-start | bytes 196616 | tf_op jit(solution)/shard_map/ppermute | solution.py:163
  42.7 1.6 %collective-permute-start.15 = (f32[576,128]{1,0:T(8,128)S(1)}, f32[576,128]{1,0:T(8,128)S(1)}, u32[]{:S(2)}, u32[]{:S(2)}) collective-permute-start(f32[576,128]{1,0:T(8,128)S(1)} %broadcast_select_fusion), channel_id=1, source_target_pairs={{0,1},{1,0},{2,3},{3,2},{4,5},{5,4},{6,7},{7,6},{8,9},{9,8},{10,11... | collective-permute-start | bytes 884744 | tf_op jit(solution)/shard_map/ppermute | solution.py:163
  43.1 2.8 %collective-permute-start.14 = (f32[576,128]{1,0:T(8,128)S(1)}, f32[576,128]{1,0:T(8,128)S(1)}, u32[]{:S(2)}, u32[]{:S(2)}) collective-permute-start(f32[576,128]{1,0:T(8,128)S(1)} %broadcast_select_fusion.1), channel_id=1, source_target_pairs={{0,1},{1,0},{2,3},{3,2},{4,5},{5,4},{6,7},{7,6},{8,9},{9,8},{10,11... | collective-permute-start | bytes 884744 | tf_op jit(solution)/shard_map/ppermute | solution.py:163
  44.3 5.9 %collective-permute-start.5 = (f32[320,128]{1,0:T(8,128)S(1)}, f32[320,128]{1,0:T(8,128)S(1)}, u32[]{:S(2)}, u32[]{:S(2)}) collective-permute-start(f32[320,128]{1,0:T(8,128)S(1)} %pad_maximum_fusion.5.pack0), channel_id=1, source_target_pairs={{0,8},{8,16},{16,24},{24,0},{1,9},{9,17},{17,25},{25,1},{2,10},{10... | collective-permute-start | bytes 491528 | tf_op jit(solution)/shard_map/ppermute | solution.py:145
  45.8 6.6 %collective-permute-start.6 = (f32[320,128]{1,0:T(8,128)S(1)}, f32[320,128]{1,0:T(8,128)S(1)}, u32[]{:S(2)}, u32[]{:S(2)}) collective-permute-start(f32[320,128]{1,0:T(8,128)S(1)} %pad_maximum_fusion.5.pack0), channel_id=1, source_target_pairs={{0,16},{8,24},{16,0},{24,8},{1,17},{9,25},{17,1},{25,9},{2,18},{10... | collective-permute-start | bytes 491528 | tf_op jit(solution)/shard_map/ppermute | solution.py:145
  48.3 8.6 %collective-permute-start.7 = (f32[320,128]{1,0:T(8,128)S(1)}, f32[320,128]{1,0:T(8,128)S(1)}, u32[]{:S(2)}, u32[]{:S(2)}) collective-permute-start(f32[320,128]{1,0:T(8,128)S(1)} %pad_maximum_fusion.5.pack0), channel_id=1, source_target_pairs={{0,24},{8,0},{16,8},{24,16},{1,25},{9,1},{17,9},{25,17},{2,26},{10... | collective-permute-start | bytes 491528 | tf_op jit(solution)/shard_map/ppermute | solution.py:145
  64.5 5.9 %collective-permute-start.16 = (f32[128,384]{1,0:T(8,128)S(1)}, f32[128,384]{1,0:T(8,128)S(1)}, u32[]{:S(2)}, u32[]{:S(2)}) collective-permute-start(f32[128,384]{1,0:T(8,128)S(1)} %get-tuple-element.17), channel_id=1, source_target_pairs={{0,8},{8,16},{16,24},{24,0},{1,9},{9,17},{17,25},{25,1},{2,10},{10... | collective-permute-start | bytes 589832 | tf_op jit(solution)/shard_map/ppermute | solution.py:145
  64.6 7.0 %collective-permute-start.17 = (f32[128,384]{1,0:T(8,128)S(1)}, f32[128,384]{1,0:T(8,128)S(1)}, u32[]{:S(2)}, u32[]{:S(2)}) collective-permute-start(f32[128,384]{1,0:T(8,128)S(1)} %get-tuple-element.18), channel_id=1, source_target_pairs={{0,16},{8,24},{16,0},{24,8},{1,17},{9,25},{17,1},{25,9},{2,18},{10... | collective-permute-start | bytes 589832 | tf_op jit(solution)/shard_map/ppermute | solution.py:145
  64.7 12.5 %collective-permute-start.18 = (f32[128,384]{1,0:T(8,128)S(1)}, f32[128,384]{1,0:T(8,128)S(1)}, u32[]{:S(2)}, u32[]{:S(2)}) collective-permute-start(f32[128,384]{1,0:T(8,128)S(1)} %get-tuple-element.19), channel_id=1, source_target_pairs={{0,24},{8,0},{16,8},{24,16},{1,25},{9,1},{17,9},{25,17},{2,26},{10... | collective-permute-start | bytes 589832 | tf_op jit(solution)/shard_map/ppermute | solution.py:145
  78.0 21.7 %all-to-all-start.1 = ((f32[8,32,384]{2,1,0:T(8,128)}), f32[8,32,384]{2,1,0:T(8,128)S(1)}, u32[]{:S(2)}, u32[]{:S(2)}) async-start(f32[8,32,384]{2,1,0:T(8,128)} %spread.1), calls=%async_computation.1 | async-start | bytes 786432 | tf_op jit(solution)/shard_map/all_to_all | solution.py:233

commit v3 on v2

--- a/solution.py
+++ b/solution.py
@@ -33,6 +33,15 @@
         return lax.dot_general(a, b, (over, ((), ())), preferred_element_type=jnp.float32)
 
     return dot(first[0], second[0]) + (dot(first[0], second[1]) + dot(first[1], second[0]))
+
+
+def brief_dot(first, second):
+    (a, b), (c, d) = split(first), split(second)
+    return jnp.dot(
+        jnp.concatenate([a, a, b], 1),
+        jnp.concatenate([c, d, c], 0),
+        preferred_element_type=jnp.float32,
+    )
 
 
 def blocks_inverse(diag_ref, inv_ref):
@@ -51,20 +60,20 @@
     size = 2
     while size < TILE:
         joined = (rows // (2 * size) == cols // (2 * size)) & (rows // size > cols // size)
-        right = [exact_dot(jnp.where(joined, d, 0.0), i) for d, i in zip(diag, inv)]
-        inv = [i - exact_dot(i, r) for i, r in zip(inv, right)]
+        right = [brief_dot(jnp.where(joined, d, 0.0), i) for d, i in zip(diag, inv)]
+        inv = [i - brief_dot(i, r) for i, r in zip(inv, right)]
         size *= 2
     inv_ref[...] = jnp.zeros((NB, NB), jnp.float32)
     for k in range(blocks):
         inv_ref[k * TILE : (k + 1) * TILE, k * TILE : (k + 1) * TILE] = inv[k]
     for k in (0, 2):
         lower = diag_ref[k, (k + 1) * TILE : (k + 2) * TILE, :]
-        inv_ref[(k + 1) * TILE : (k + 2) * TILE, k * TILE : (k + 1) * TILE] = -exact_dot(
-            inv[k + 1], exact_dot(lower, inv[k])
+        inv_ref[(k + 1) * TILE : (k + 2) * TILE, k * TILE : (k + 1) * TILE] = -brief_dot(
+            inv[k + 1], brief_dot(lower, inv[k])
         )
     half = NB // 2
     corner = jnp.concatenate([diag_ref[0, half:, :], diag_ref[1, half:, :]], axis=1)
-    inv_ref[half:, :half] = -exact_dot(inv_ref[half:, half:], exact_dot(corner, inv_ref[:half, :half]))
+    inv_ref[half:, :half] = -brief_dot(inv_ref[half:, half:], brief_dot(corner, inv_ref[:half, :half]))
 
 
 def solve_kernel(
@@ -84,10 +93,10 @@
                 at += 32
         for zl in range(4):
             start = pl.multiple_of((zl * 4 + (x - step) % 4) * 32, 32)
-            line = lefts[step][zl * 32 : (zl + 1) * 32, :]
             eye = (rows + start == cols).astype(jnp.float32)
-            right[pl.ds(start, 32), : 2 * TILE] = line[:, : 2 * TILE]
-            right[pl.ds(start, 32), 2 * TILE :] = jnp.where(owner == 1, eye, line[:, 2 * TILE :])
+            right[pl.ds(start, 32), :TILE] = lefts[step][zl, 0]
+            right[pl.ds(start, 32), TILE : 2 * TILE] = lefts[step][zl, 1]
+            right[pl.ds(start, 32), 2 * TILE :] = jnp.where(owner == 1, eye, lefts[step][zl, 2])
     blocks_inverse(diag, inv)
     inverse = split(inv[...])
     solved = split_dot(inverse, split(right[...]))
@@ -97,21 +106,22 @@
     for step, part in enumerate((part0, part1, part2, part3)):
         for zl in range(4):
             start = pl.multiple_of((zl * 4 + (x + step) % 4) * 32, 32)
-            part[zl * 32 : (zl + 1) * 32, :] = partial[pl.ds(start, 32), :]
+            for e in range(3):
+                part[zl, e] = partial[pl.ds(start, 32), e * TILE : (e + 1) * TILE]
 
 
 def spread_kernel(part0, part1, part2, part3, out):
-    total = (part0[...] + part1[...]) + (part2[...] + part3[...])
     for zl in range(4):
-        out[zl] = jnp.zeros((32, WIDE), jnp.float32)
-        out[4 + zl] = total[zl * 32 : (zl + 1) * 32, :]
+        total = (part0[zl] + part1[zl]) + (part2[zl] + part3[zl])
+        out[(zl + 2) % 4] = total[:, :16]
+        out[4 + zl] = total[:, 16:]
 
 
 def spread_sum(*parts):
     parts = [pltpu.with_memory_space_constraint(p, pltpu.VMEM) for p in parts]
     return pl.pallas_call(
         spread_kernel,
-        out_shape=pltpu.VMEM((8, 32, WIDE), jnp.float32),
+        out_shape=pltpu.VMEM((8, 3, 16, TILE), jnp.float32),
         in_specs=[pl.BlockSpec(memory_space=pltpu.VMEM)] * 4,
         out_specs=pl.BlockSpec(memory_space=pltpu.VMEM),
         compiler_params=pltpu.CompilerParams(vmem_limit_bytes=8 << 20),
@@ -119,9 +129,44 @@
     )(*parts)
 
 
+def finish_kernel(place, base, tops, share, other, out, stage, sem):
+    low, owner, gap = place[0], place[1], place[2]
+
+    @pl.when(low == 1)
+    def _():
+        change = jnp.concatenate([other[...], share[...]], axis=1)
+        away = (
+            lax.broadcasted_iota(jnp.int32, (32, TILE), 0)
+            - lax.broadcasted_iota(jnp.int32, (32, TILE), 1)
+            + gap
+        )
+        halved = jnp.where(away > 0, 1.0, jnp.where(away == 0, 0.5, 0.0)) * change[2]
+        stage[0] = tops[0] - change[0]
+        stage[1] = tops[1] - change[1]
+        stage[2] = jnp.where(owner == 1, halved, tops[2] - change[2])
+        copy = pltpu.make_async_copy(stage, out.at[0], sem)
+        copy.start()
+        copy.wait()
+
+
+def finished(place, base, tops, share, other):
+    small = [pltpu.with_memory_space_constraint(a, pltpu.VMEM) for a in (tops, share, other)]
+    return pl.pallas_call(
+        finish_kernel,
+        out_shape=jax.ShapeDtypeStruct(base.shape, jnp.float32),
+        in_specs=[pl.BlockSpec(memory_space=pltpu.SMEM), pl.BlockSpec(memory_space=pl.ANY)]
+        + [pl.BlockSpec(memory_space=pltpu.VMEM)] * 3,
+        out_specs=pl.BlockSpec(memory_space=pl.ANY),
+        scratch_shapes=[pltpu.VMEM((3, 32, TILE), jnp.float32), pltpu.SemaphoreType.DMA],
+        input_output_aliases={1: 0},
+        compiler_params=pltpu.CompilerParams(vmem_limit_bytes=4 << 20),
+        name="finish",
+    )(place, base, *small)
+
+
 def solved_parts(place, *arrays):
     arrays = [pltpu.with_memory_space_constraint(a, pltpu.VMEM) for a in arrays]
-    part = pltpu.VMEM((TILE, WIDE), jnp.float32)
+    part = pltpu.VMEM((4, 3, 32, TILE), jnp.float32)
     return pl.pallas_call(
         solve_kernel,
         out_shape=(pltpu.VMEM((NB, WIDE), jnp.float32),) + (part,) * 4,
@@ -139,6 +184,24 @@
     )(place, *arrays)
 
 
+def copies_kernel(source, out):
+    for z in range(8):
+        out[z] = source[0]
+
+
+def copies(source):
+    block = source.shape[1:]
+    return pl.pallas_call(
+        copies_kernel,
+        grid=(1,),
+        out_shape=pltpu.VMEM((8, *block), jnp.float32),
+        in_specs=[pl.BlockSpec((1, *block), lambda i: (0, 0, 0, 0))],
+        out_specs=pl.BlockSpec(memory_space=pltpu.VMEM),
+        compiler_params=pltpu.CompilerParams(vmem_limit_bytes=4 << 20),
+        name="copies",
+    )(pltpu.with_memory_space_constraint(source, pltpu.HBM))
+
+
 def over_x(block):
     blocks = block if isinstance(block, tuple) else (block,) * 3
     return tuple(
@@ -180,35 +243,30 @@
     return ordered(near, rest, swap(near), swap(rest))
 
 
-def to_all(block, axis):
-    size = lax.axis_size(axis)
-    return lax.all_to_all(
-        jnp.broadcast_to(block[None], (size, *block.shape)), axis, 0, 0, tiled=True
-    )
-
-
 def step(factor, adjoint):
     row, x = lax.axis_index(ROW), lax.axis_index("x")
     col = lax.axis_index("y") * 2 + lax.axis_index("k")
     low = lax.axis_index("zh") == 1
     owner = col >= 4
-    f0, f1, f2 = (factor[:, :, e, :].reshape(288, TILE) for e in range(3))
-    a0, a1, a2 = (adjoint[:, :, e, :].reshape(288, TILE) for e in range(3))
+    factor, adjoint = factor.transpose(0, 2, 1, 3), adjoint.transpose(0, 2, 1, 3)
+    f2, a2 = factor[:, 2].reshape(288, TILE), adjoint[:, 2].reshape(288, TILE)
     own_rows = row * 32 + jnp.arange(32, dtype=jnp.int32)
     own_cols = col * TILE + jnp.arange(TILE, dtype=jnp.int32)
     a2_top = jnp.where(own_cols[None, :] > own_rows[:, None], 0.0, a2[:32])
     a2 = jnp.concatenate([a2_top, a2[32:]], 0)
 
-    tops_l = jnp.concatenate([f0[:32], f1[:32], f2[:32]], 1)
-    lines = to_all(tops_l, ("zh", "zl"))[4:].reshape(TILE, WIDE)
-    sent = over_y(jnp.concatenate([a2, f2], 0))
-    last = lines[:, 2 * TILE :]
-    near, rest = own_pair(last, *over_y(last))
+    lines = lax.all_to_all(copies(factor), ("zh", "zl"), 0, 0, tiled=True)[4:]
+    both = jnp.concatenate([a2, f2], 0)
+    near = lax.ppermute(both, "y", [(2, 1), (3, 0)])
+    across = lax.ppermute(both, "y", [(2, 3), (3, 2)])
+    sent = near, across, lax.ppermute(both, "y", [(2, 0), (3, 1)])
+    last = lines[:, 2].reshape(TILE, TILE)
+    low_block, rest = own_pair(last, *over_y(last))
     lefts = (lines, *over_x(lines))
-    quads = ordered(near, rest, swap(near), swap(rest))
+    quads = ordered(low_block, rest, swap(low_block), swap(rest))
     pack = jnp.concatenate([quads[c][32 * c :] for c in range(4)], 0)
     packs = (pack, *over_x(pack))
-    panels = panel_blocks(jnp.concatenate([a2, f2], 0), sent, near)
+    panels = panel_blocks(both, sent, low_block)
     adj_panel = jnp.concatenate([p[:288] for p in panels], 1)
     fac_panel = jnp.concatenate([p[288:] for p in panels], 1)
 
@@ -222,7 +280,8 @@
     middle = -jnp.where(
         kept, close_dot(first, second, over_rows), close_dot(second, first, over_rows)
     )
-    below = jnp.concatenate([f0[32:], f1[32:], jnp.where(owner, 0.0, f2[32:])], 1)
+    f0, f1 = (factor[1:, e].reshape(256, TILE) for e in range(2))
+    below = jnp.concatenate([f0, f1, jnp.where(owner, 0.0, f2[32:])], 1)
     outer = close_dot(weights, below, over_rows)
     place = jnp.stack(
         [x, owner.astype(jnp.int32), col * TILE - 512]
@@ -230,24 +289,18 @@
     solved, *parts = solved_parts(place, *packs, *lefts, outer, middle)
     moved = over_x(tuple(parts[1:]))
     spread = spread_sum(parts[0], *moved)
-    change = lax.all_to_all(spread, ("zh", "zl"), 0, 0, tiled=True).sum(axis=0)
-
-    update = close_dot(weights, solved)
-    tops = jnp.concatenate([a0[:32], a1[:32], a2_top], 1)
-    gap = own_rows[:, None] - own_cols[None, :]
-    halved = jnp.where(gap > 0, 1.0, jnp.where(gap == 0, 0.5, 0.0)) * change[:, 2 * TILE :]
-    new_diag = jnp.where(owner, halved, tops[:, 2 * TILE :] - change[:, 2 * TILE :])
-    new_top = jnp.concatenate([tops[:, : 2 * TILE] - change[:, : 2 * TILE], new_diag], 1)
-    new_top = jnp.where(low, new_top, tops)
-    new_below = jnp.concatenate(
-        [
-            a0[32:] - update[:, :TILE],
-            a1[32:] - update[:, TILE : 2 * TILE],
-            jnp.where(owner, update[:, 2 * TILE :], a2[32:] - update[:, 2 * TILE :]),
-        ],
-        1,
-    )
-    return jnp.concatenate([new_top, new_below], 0).reshape(9, 32, 3, TILE)
+    share = lax.all_to_all(spread, ("zh", "zl"), 0, 0, tiled=True).sum(axis=0)
+    other = lax.ppermute(share, ("zh", "zl"), [(i, 4 + (i + 2) % 4) for i in range(4)])
+
+    update = close_dot(weights, solved).reshape(8, 32, 3, TILE).transpose(0, 2, 1, 3)
+    tops = jnp.concatenate([adjoint[0, :2], a2_top[None]], 0)
+    new_col = jnp.where(owner, update[:, 2], adjoint[1:, 2] - update[:, 2])
+    below = jnp.concatenate([adjoint[1:, :2] - update[:, :2], new_col[:, None]], 1)
+    base = jnp.concatenate([tops[None], below], 0)
+    end_place = jnp.stack(
+        [low.astype(jnp.int32), owner.astype(jnp.int32), row * 32 - col * TILE]
+    ).astype(jnp.int32)
+    return finished(end_place, base, tops, share, other).transpose(0, 2, 1, 3)
 
 
 def solution(mesh):

time: 101 us -> 103 us (1.020)
  the two profiles are of different devices: /device:TPU:7 before, /device:TPU:6 now
where the time goes in v3:
time: 103 us
  waiting for transfers between devices  54.5 us (53%)
  starting transfers between devices  31.4 us (30%)
  Pallas kernels  9.36 us (9%)
  matrix products  3.31 us (3%)
  local copies, waits for them, and re-layouts  2.25 us (2%)
  other arithmetic  1.58 us (2%)
    ppermute x9, waiting for transfers between devices, over_x(): lax.ppermute(b, 'x', [(i, (i + s) % 4) for i in range(4)])  14.9 us
    all_to_all x1, waiting for transfers between devices, step(): lines = lax.all_to_all(copies(factor), ('zh', 'zl'), 0, 0, tiled=True)[4:]  14.6 us
    all_to_all x1, waiting for transfers between devices, step(): share = lax.all_to_all(spread, ('zh', 'zl'), 0, 0, tiled=True).sum(axis=0)  10.7 us
    ppermute x9, starting transfers between devices, over_x(): lax.ppermute(b, 'x', [(i, (i + s) % 4) for i in range(4)])  9.55 us
    ppermute x1, waiting for transfers between devices, over_y(): near = lax.ppermute(block, 'y', [(2, 1), (3, 0)])  9.07 us
    all_to_all x1, starting transfers between devices, step(): lines = lax.all_to_all(copies(factor), ('zh', 'zl'), 0, 0, tiled=True)[4:]  8.6 us
    pallas_call x1, Pallas kernels, solved_parts(): pl.pallas_call(solve_kernel, out_shape=(pltpu.VMEM((NB, WIDE), jnp.float3...  6.52 us
    all_to_all x1, starting transfers between devices, step(): share = lax.all_to_all(spread, ('zh', 'zl'), 0, 0, tiled=True).sum(axis=0)  3.39 us
  transfers between devices with their start and end apart: 22, of which 13 were waited for; matrix products, arithmetic and copies ran while one was open for 5% of the time, Pallas kernels for 2%

profile of v3, /device:TPU:6, one launch (start us, length us, event | category | flops | bytes accessed | tf_op | source)
XLA Modules:
  0.0 102.9 jit_solution(10727018310970697753)
XLA Ops:
  0.0 1.0 slice.131
  1.0 0.9 slice.130
  2.1 1.3 %collective-permute-start = (f32[576,128]{1,0:T(8,128)S(1)}, f32[576,128]{1,0:T(8,128)S(1)}, u32[]{:S(2)}, u32[]{:S(2)}) collective-permute-start(f32[576,128]{1,0:T(8,128)S(1)} %pad_maximum_fusion.4), channel_id=1, source_target_pairs={{4,2},{6,0},{5,3},{7,1},{12,10},{14,8},{13,11},{15,9},{20,18},{22,... | collective-permute-start | bytes 884744 | tf_op jit(solution)/shard_map/ppermute | solution.py:260
  3.4 0.7 collective-permute-start.1
  4.0 1.3 %collective-permute-start.2 = (f32[576,128]{1,0:T(8,128)S(1)}, f32[576,128]{1,0:T(8,128)S(1)}, u32[]{:S(2)}, u32[]{:S(2)}) collective-permute-start(f32[576,128]{1,0:T(8,128)S(1)} %pad_maximum_fusion.4), channel_id=1, source_target_pairs={{4,0},{6,2},{5,1},{7,3},{12,8},{14,10},{13,9},{15,11},{20,16},{22,... | collective-permute-start | bytes 884744 | tf_op jit(solution)/shard_map/ppermute | solution.py:262
  5.3 1.6 %copies.1 = f32[8,3,32,128]{3,2,1,0:T(8,128)} custom-call(f32[9,3,32,128]{3,2,1,0:T(8,128)} %bitcast.29), custom_call_target="tpu_custom_call" | custom-call | tf_op jit(solution)/shard_map/copies/pallas_call | solution.py:194
  6.9 8.6 %all-to-all-start = ((f32[8,3,32,128]{3,2,1,0:T(8,128)}), f32[8,3,32,128]{3,2,1,0:T(8,128)S(1)}, u32[]{:S(2)}, u32[]{:S(2)}) async-start(f32[8,3,32,128]{3,2,1,0:T(8,128)} %copies.1), calls=%async_computation | async-start | bytes 786432 | tf_op jit(solution)/shard_map/all_to_all | solution.py:258
  15.7 14.6 %all-to-all-done = f32[8,3,32,128]{3,2,1,0:T(8,128)S(1)} async-done(((f32[8,3,32,128]{3,2,1,0:T(8,128)}), f32[8,3,32,128]{3,2,1,0:T(8,128)S(1)}, u32[]{:S(2)}, u32[]{:S(2)}) %all-to-all-start) | async-done | bytes 393248 | tf_op jit(solution)/shard_map/all_to_all | solution.py:258
  30.2 0.7 collective-permute-start.3
  31.0 1.3 %collective-permute-start.4 = (f32[128,128]{1,0:T(8,128)S(1)}, f32[128,128]{1,0:T(8,128)S(1)}, u32[]{:S(2)}, u32[]{:S(2)}) collective-permute-start(f32[128,128]{1,0:T(8,128)S(1)} %bitcast.47), channel_id=1, source_target_pairs={{4,2},{6,0},{5,3},{7,1},{12,10},{14,8},{13,11},{15,9},{20,18},{22,... | collective-permute-start | bytes 196616 | tf_op jit(solution)/shard_map/ppermute | solution.py:214
  32.3 1.3 %collective-permute-start.8 = (f32[128,128]{1,0:T(8,128)S(1)}, f32[128,128]{1,0:T(8,128)S(1)}, u32[]{:S(2)}, u32[]{:S(2)}) collective-permute-start(f32[128,128]{1,0:T(8,128)S(1)} %bitcast.48), channel_id=1, source_target_pairs={{4,0},{6,2},{5,1},{7,3},{12,8},{14,10},{13,9},{15,11},{20,16},{22,... | collective-permute-start | bytes 196616 | tf_op jit(solution)/shard_map/ppermute | solution.py:216
  33.7 9.1 %collective-permute-done.4 = f32[128,128]{1,0:T(8,128)S(1)} collective-permute-done((f32[128,128]{1,0:T(8,128)S(1)}, f32[128,128]{1,0:T(8,128)S(1)}, u32[]{:S(2)}, u32[]{:S(2)}) %collective-permute-start.4) | collective-permute-done | bytes 65568 | tf_op jit(solution)/shard_map/ppermute | solution.py:214
  42.7 0.5 collective-permute-start.13
  43.2 2.9 %collective-permute-done.8 = f32[128,128]{1,0:T(8,128)S(1)} collective-permute-done((f32[128,128]{1,0:T(8,128)S(1)}, f32[128,128]{1,0:T(8,128)S(1)}, u32[]{:S(2)}, u32[]{:S(2)}) %collective-permute-start.8) | collective-permute-done | bytes 65568 | tf_op jit(solution)/shard_map/ppermute | solution.py:216
  46.1 1.4 %collective-permute-start.14 = (f32[4,3,32,128]{3,2,1,0:T(8,128)S(1)}, f32[4,3,32,128]{3,2,1,0:T(8,128)S(1)}, u32[]{:S(2)}, u32[]{:S(2)}) collective-permute-start(f32[4,3,32,128]{3,2,1,0:T(8,128)S(1)} %slice.144.left0), channel_id=1, source_target_pairs={{0,16},{8,24},{16,0},{24,8},{1,17},{9,25},{17,1},{25,9},{2,18},{10... | collective-permute-start | bytes 589832 | tf_op jit(solution)/shard_map/ppermute | solution.py:208
  47.5 0.1 collective-permute-start.15
  47.6 0.1 collective-permute-start.7
  47.7 0.5 collective-permute-start.9
  48.3 0.7 collective-permute-done.7
  49.0 0.2 collective-permute-start.5
  49.1 0.4 collective-permute-start.6
  49.6 1.0 collective-permute-done.5
  50.5 3.1 %collective-permute-start.10 = (f32[320,128]{1,0:T(8,128)S(1)}, f32[320,128]{1,0:T(8,128)S(1)}, u32[]{:S(2)}, u32[]{:S(2)}) collective-permute-start(f32[320,128]{1,0:T(8,128)S(1)} %pad_maximum_fusion.5.pack0), channel_id=1, source_target_pairs={{0,8},{8,16},{16,24},{24,0},{1,9},{9,17},{17,25},{25,1},{2,10},{10... | collective-permute-start | bytes 491528 | tf_op jit(solution)/shard_map/ppermute | solution.py:208
  53.7 0.9 collective-permute-start.11
  54.6 0.1 broadcast_select_fusion.9
  54.9 1.0 %fusion.2 = f32[512,512]{1,0:T(8,128)S(1)} fusion(f32[256,512]{1,0:T(8,128)S(1)} %slice.137, f32[32,512]{1,0:T(8,128)S(1)} %maximum_multiply_fusion, f32[288,128]{1,0:T(8,128)S(1)} %get-tuple-element.48, f32[288,128]{1,0:T(8,128)S(1)} %get-tuple-element.38, f32[288,128]{1,0:T(8,128)S(1)} %get-tuple-element.46, f32[288,128]{1,0:T(8,128)S(1)} %get-tuple-element.34, ...), kind=kOutput, calls=%fused_computation.10 | convolution fusion | flops 454459392 | bytes 2293760 | tf_op jit(solution)/shard_map/dot_general | solution.py:16
  56.0 1.0 %fusion.middle = f32[512,512]{1,0:T(8,128)S(1)} fusion(f32[512,512]{1,0:T(8,128)S(1)} %fusion.2, f32[256,512]{1,0:T(8,128)S(1)} %slice.137, f32[32,512]{1,0:T(8,128)S(1)} %maximum_multiply_fusion, f32[288,128]{1,0:T(8,128)S(1)} %get-tuple-element.48, f32[288,128]{1,0:T(8,128)S(1)} %get-tuple-element.38, f32[288,128]{1,0:T(8,128)S(1)} %get-tuple-element.46, ...), kind=kOutput, calls=%fused_computation.1 | convolution fusion | flops 455245824 | bytes 3342336 | tf_op jit(solution)/shard_map/dot_general | solution.py:16
  57.1 1.1 %collective-permute-start.12 = (f32[320,128]{1,0:T(8,128)S(1)}, f32[320,128]{1,0:T(8,128)S(1)}, u32[]{:S(2)}, u32[]{:S(2)}) collective-permute-start(f32[320,128]{1,0:T(8,128)S(1)} %pad_maximum_fusion.5.pack0), channel_id=1, source_target_pairs={{0,24},{8,0},{16,8},{24,16},{1,25},{9,1},{17,9},{25,17},{2,26},{10... | collective-permute-start | bytes 491528 | tf_op jit(solution)/shard_map/ppermute | solution.py:208
  58.2 0.6 fusion.3.outer
  58.8 2.2 %collective-permute-done.10.pack1 = f32[320,128]{1,0:T(8,128)S(1)} collective-permute-done((f32[320,128]{1,0:T(8,128)S(1)}, f32[320,128]{1,0:T(8,128)S(1)}, u32[]{:S(2)}, u32[]{:S(2)}) %collective-permute-start.10) | collective-permute-done | bytes 163872 | tf_op jit(solution)/shard_map/ppermute | solution.py:208
  61.0 1.0 collective-permute-done.11.pack2
  61.9 3.0 %collective-permute-done.12.pack3 = f32[320,128]{1,0:T(8,128)S(1)} collective-permute-done((f32[320,128]{1,0:T(8,128)S(1)}, f32[320,128]{1,0:T(8,128)S(1)}, u32[]{:S(2)}, u32[]{:S(2)}) %collective-permute-start.12) | collective-permute-done | bytes 163872 | tf_op jit(solution)/shard_map/ppermute | solution.py:208
  64.9 6.5 %solve.1 = (f32[512,384]{1,0:T(8,128)S(1)}, f32[4,3,32,128]{3,2,1,0:T(8,128)S(1)}, f32[4,3,32,128]{3,2,1,0:T(8,128)S(1)}, f32[4,3,32,128]{3,2,1,0:T(8,128)S(1)}, f32[4,3,32,128]{3,2,1,0:T(8,128)S(1)}) custom-call(s32[3]{0:T(128)S(1)} %pad_add_fusion.1.place, f32[320,128]{1,0:T(8,128)S(1)} %pad_maximum_fusion.5.pack0, ...), custom_call_target="tpu_custom_call" | custom-call | tf_op jit(solution)/shard_map/solve/pallas_call | solution.py:170
  71.4 0.4 collective-permute-start.16
  71.8 1.0 collective-permute-start.17
  72.9 1.0 collective-permute-start.18
  73.9 0.6 fusion.18
  74.5 0.2 reshape.70
  74.7 4.6 %collective-permute-done.16.part1 = f32[4,3,32,128]{3,2,1,0:T(8,128)S(1)} collective-permute-done((f32[4,3,32,128]{3,2,1,0:T(8,128)S(1)}, f32[4,3,32,128]{3,2,1,0:T(8,128)S(1)}, u32[]{:S(2)}, u32[]{:S(2)}) %collective-permute-start.16) | collective-permute-done | bytes 196640 | tf_op jit(solution)/shard_map/ppermute | solution.py:208
  79.3 1.9 %collective-permute-done.17.part2 = f32[4,3,32,128]{3,2,1,0:T(8,128)S(1)} collective-permute-done((f32[4,3,32,128]{3,2,1,0:T(8,128)S(1)}, f32[4,3,32,128]{3,2,1,0:T(8,128)S(1)}, u32[]{:S(2)}, u32[]{:S(2)}) %collective-permute-start.17) | collective-permute-done | bytes 196640 | tf_op jit(solution)/shard_map/ppermute | solution.py:208
  81.1 2.4 %collective-permute-done.18.part3 = f32[4,3,32,128]{3,2,1,0:T(8,128)S(1)} collective-permute-done((f32[4,3,32,128]{3,2,1,0:T(8,128)S(1)}, f32[4,3,32,128]{3,2,1,0:T(8,128)S(1)}, u32[]{:S(2)}, u32[]{:S(2)}) %collective-permute-start.18) | collective-permute-done | bytes 196640 | tf_op jit(solution)/shard_map/ppermute | solution.py:208
  83.5 0.7 spread.1
  84.2 3.4 %all-to-all-start.1 = ((f32[8,3,16,128]{3,2,1,0:T(8,128)}), f32[8,3,16,128]{3,2,1,0:T(8,128)S(1)}, u32[]{:S(2)}, u32[]{:S(2)}) async-start(f32[8,3,16,128]{3,2,1,0:T(8,128)} %spread.1), calls=%async_computation.1 | async-start | bytes 393216 | tf_op jit(solution)/shard_map/all_to_all | solution.py:292
  87.7 10.7 %all-to-all-done.1 = f32[8,3,16,128]{3,2,1,0:T(8,128)S(1)} async-done(((f32[8,3,16,128]{3,2,1,0:T(8,128)}), f32[8,3,16,128]{3,2,1,0:T(8,128)S(1)}, u32[]{:S(2)}, u32[]{:S(2)}) %all-to-all-start.1) | async-done | bytes 196640 | tf_op jit(solution)/shard_map/all_to_all | solution.py:292
  98.4 2.2 %collective-permute-start.19 = (f32[3,16,128]{2,1,0:T(8,128)S(1)}, f32[3,16,128]{2,1,0:T(8,128)S(1)}, u32[]{:S(2)}, u32[]{:S(2)}) collective-permute-start(f32[3,16,128]{2,1,0:T(8,128)S(1)} %reduce_sum.9.share), channel_id=1, source_target_pairs={{0,192},{32,224},{64,128},{96,160},{1,193},{33,225},{65,129},{97,1... | collective-permute-start | bytes 73736 | tf_op jit(solution)/shard_map/ppermute | solution.py:293
  100.7 0.8 maximum_maximum_fusion.base
  101.5 0.7 collective-permute-done.19.other
  102.2 0.6 finish.1
  (43 shorter events, 0.9 us)
Async XLA Ops:
  0.0 2.0 %copy-start.1 = (f32[9,32,3,128]{3,1,2,0:T(8,128)S(1)}, f32[9,32,3,128]{3,1,2,0:T(8,128)}, u32[]{:S(2)}) copy-start(f32[9,32,3,128]{3,1,2,0:T(8,128)} %param.3) | copy-start | bytes 1327108
  2.1 45.4 %collective-permute-start = (f32[576,128]{1,0:T(8,128)S(1)}, f32[576,128]{1,0:T(8,128)S(1)}, u32[]{:S(2)}, u32[]{:S(2)}) collective-permute-start(f32[576,128]{1,0:T(8,128)S(1)} %pad_maximum_fusion.4), channel_id=1, source_target_pairs={{4,2},{6,0},{5,3},{7,1},{12,10},{14,8},{13,11},{15,9},{20,18},{22,... | collective-permute-start | bytes 884744 | tf_op jit(solution)/shard_map/ppermute | solution.py:260
  3.4 44.2 %collective-permute-start.1 = (f32[576,128]{1,0:T(8,128)S(1)}, f32[576,128]{1,0:T(8,128)S(1)}, u32[]{:S(2)}, u32[]{:S(2)}) collective-permute-start(f32[576,128]{1,0:T(8,128)S(1)} %pad_maximum_fusion.4), channel_id=1, source_target_pairs={{4,6},{6,4},{5,7},{7,5},{12,14},{14,12},{13,15},{15,13},{20,22},{2... | collective-permute-start | bytes 884744 | tf_op jit(solution)/shard_map/ppermute | solution.py:261
  4.0 43.7 %collective-permute-start.2 = (f32[576,128]{1,0:T(8,128)S(1)}, f32[576,128]{1,0:T(8,128)S(1)}, u32[]{:S(2)}, u32[]{:S(2)}) collective-permute-start(f32[576,128]{1,0:T(8,128)S(1)} %pad_maximum_fusion.4), channel_id=1, source_target_pairs={{4,0},{6,2},{5,1},{7,3},{12,8},{14,10},{13,9},{15,11},{20,16},{22,... | collective-permute-start | bytes 884744 | tf_op jit(solution)/shard_map/ppermute | solution.py:262
  6.9 8.7 %copy-start = (f32[9,32,3,128]{3,1,2,0:T(8,128)S(1)}, f32[9,32,3,128]{3,1,2,0:T(8,128)}, u32[]{:S(2)}) copy-start(f32[9,32,3,128]{3,1,2,0:T(8,128)} %param.2) | copy-start | bytes 1327108
  6.9 23.3 %all-to-all-start = ((f32[8,3,32,128]{3,2,1,0:T(8,128)}), f32[8,3,32,128]{3,2,1,0:T(8,128)S(1)}, u32[]{:S(2)}, u32[]{:S(2)}) async-start(f32[8,3,32,128]{3,2,1,0:T(8,128)} %copies.1), calls=%async_computation | async-start | bytes 786432 | tf_op jit(solution)/shard_map/all_to_all | solution.py:258
  30.2 2.0 %collective-permute-start.3 = (f32[128,128]{1,0:T(8,128)S(1)}, f32[128,128]{1,0:T(8,128)S(1)}, u32[]{:S(2)}, u32[]{:S(2)}) collective-permute-start(f32[128,128]{1,0:T(8,128)S(1)} %bitcast.46), channel_id=1, source_target_pairs={{4,6},{6,4},{5,7},{7,5},{12,14},{14,12},{13,15},{15,13},{20,22},{2... | collective-permute-start | bytes 196616 | tf_op jit(solution)/shard_map/ppermute | solution.py:215
  31.0 11.8 %collective-permute-start.4 = (f32[128,128]{1,0:T(8,128)S(1)}, f32[128,128]{1,0:T(8,128)S(1)}, u32[]{:S(2)}, u32[]{:S(2)}) collective-permute-start(f32[128,128]{1,0:T(8,128)S(1)} %bitcast.47), channel_id=1, source_target_pairs={{4,2},{6,0},{5,3},{7,1},{12,10},{14,8},{13,11},{15,9},{20,18},{22,... | collective-permute-start | bytes 196616 | tf_op jit(solution)/shard_map/ppermute | solution.py:214
  32.3 13.8 %collective-permute-start.8 = (f32[128,128]{1,0:T(8,128)S(1)}, f32[128,128]{1,0:T(8,128)S(1)}, u32[]{:S(2)}, u32[]{:S(2)}) collective-permute-start(f32[128,128]{1,0:T(8,128)S(1)} %bitcast.48), channel_id=1, source_target_pairs={{4,0},{6,2},{5,1},{7,3},{12,8},{14,10},{13,9},{15,11},{20,16},{22,... | collective-permute-start | bytes 196616 | tf_op jit(solution)/shard_map/ppermute | solution.py:216
  42.7 14.3 %collective-permute-start.13 = (f32[4,3,32,128]{3,2,1,0:T(8,128)S(1)}, f32[4,3,32,128]{3,2,1,0:T(8,128)S(1)}, u32[]{:S(2)}, u32[]{:S(2)}) collective-permute-start(f32[4,3,32,128]{3,2,1,0:T(8,128)S(1)} %slice.144.left0), channel_id=1, source_target_pairs={{0,8},{8,16},{16,24},{24,0},{1,9},{9,17},{17,25},{25,1},{2,10},{10... | collective-permute-start | bytes 589832 | tf_op jit(solution)/shard_map/ppermute | solution.py:208
  46.1 12.7 %collective-permute-start.14 = (f32[4,3,32,128]{3,2,1,0:T(8,128)S(1)}, f32[4,3,32,128]{3,2,1,0:T(8,128)S(1)}, u32[]{:S(2)}, u32[]{:S(2)}) collective-permute-start(f32[4,3,32,128]{3,2,1,0:T(8,128)S(1)} %slice.144.left0), channel_id=1, source_target_pairs={{0,16},{8,24},{16,0},{24,8},{1,17},{9,25},{17,1},{25,9},{2,18},{10... | collective-permute-start | bytes 589832 | tf_op jit(solution)/shard_map/ppermute | solution.py:208
  47.5 11.3 %collective-permute-start.15 = (f32[4,3,32,128]{3,2,1,0:T(8,128)S(1)}, f32[4,3,32,128]{3,2,1,0:T(8,128)S(1)}, u32[]{:S(2)}, u32[]{:S(2)}) collective-permute-start(f32[4,3,32,128]{3,2,1,0:T(8,128)S(1)} %slice.144.left0), channel_id=1, source_target_pairs={{0,24},{8,0},{16,8},{24,16},{1,25},{9,1},{17,9},{25,17},{2,26},{10... | collective-permute-start | bytes 589832 | tf_op jit(solution)/shard_map/ppermute | solution.py:208
  47.6 1.3 %collective-permute-start.7 = (f32[128,128]{1,0:T(8,128)S(1)}, f32[128,128]{1,0:T(8,128)S(1)}, u32[]{:S(2)}, u32[]{:S(2)}) collective-permute-start(f32[128,128]{1,0:T(8,128)S(1)} %get-tuple-element.25), channel_id=1, source_target_pairs={{0,1},{1,0},{2,3},{3,2},{4,5},{5,4},{6,7},{7,6},{8,9},{9,8},{10,11... | collective-permute-start | bytes 196616 | tf_op jit(solution)/shard_map/ppermute | solution.py:226
  47.7 1.4 %collective-permute-start.9 = (f32[128,128]{1,0:T(8,128)S(1)}, f32[128,128]{1,0:T(8,128)S(1)}, u32[]{:S(2)}, u32[]{:S(2)}) collective-permute-start(f32[128,128]{1,0:T(8,128)S(1)} %get-tuple-element.26), channel_id=1, source_target_pairs={{0,1},{1,0},{2,3},{3,2},{4,5},{5,4},{6,7},{7,6},{8,9},{9,8},{10,11... | collective-permute-start | bytes 196616 | tf_op jit(solution)/shard_map/ppermute | solution.py:226
  49.0 1.6 %collective-permute-start.5 = (f32[576,128]{1,0:T(8,128)S(1)}, f32[576,128]{1,0:T(8,128)S(1)}, u32[]{:S(2)}, u32[]{:S(2)}) collective-permute-start(f32[576,128]{1,0:T(8,128)S(1)} %broadcast_select_fusion.1), channel_id=1, source_target_pairs={{0,1},{1,0},{2,3},{3,2},{4,5},{5,4},{6,7},{7,6},{8,9},{9,8},{10,11... | collective-permute-start | bytes 884744 | tf_op jit(solution)/shard_map/ppermute | solution.py:226
  49.1 4.6 %collective-permute-start.6 = (f32[576,128]{1,0:T(8,128)S(1)}, f32[576,128]{1,0:T(8,128)S(1)}, u32[]{:S(2)}, u32[]{:S(2)}) collective-permute-start(f32[576,128]{1,0:T(8,128)S(1)} %broadcast_select_fusion), channel_id=1, source_target_pairs={{0,1},{1,0},{2,3},{3,2},{4,5},{5,4},{6,7},{7,6},{8,9},{9,8},{10,11... | collective-permute-start | bytes 884744 | tf_op jit(solution)/shard_map/ppermute | solution.py:226
  50.5 10.4 %collective-permute-start.10 = (f32[320,128]{1,0:T(8,128)S(1)}, f32[320,128]{1,0:T(8,128)S(1)}, u32[]{:S(2)}, u32[]{:S(2)}) collective-permute-start(f32[320,128]{1,0:T(8,128)S(1)} %pad_maximum_fusion.5.pack0), channel_id=1, source_target_pairs={{0,8},{8,16},{16,24},{24,0},{1,9},{9,17},{17,25},{25,1},{2,10},{10... | collective-permute-start | bytes 491528 | tf_op jit(solution)/shard_map/ppermute | solution.py:208
  53.7 8.3 %collective-permute-start.11 = (f32[320,128]{1,0:T(8,128)S(1)}, f32[320,128]{1,0:T(8,128)S(1)}, u32[]{:S(2)}, u32[]{:S(2)}) collective-permute-start(f32[320,128]{1,0:T(8,128)S(1)} %pad_maximum_fusion.5.pack0), channel_id=1, source_target_pairs={{0,16},{8,24},{16,0},{24,8},{1,17},{9,25},{17,1},{25,9},{2,18},{10... | collective-permute-start | bytes 491528 | tf_op jit(solution)/shard_map/ppermute | solution.py:208
  57.1 7.8 %collective-permute-start.12 = (f32[320,128]{1,0:T(8,128)S(1)}, f32[320,128]{1,0:T(8,128)S(1)}, u32[]{:S(2)}, u32[]{:S(2)}) collective-permute-start(f32[320,128]{1,0:T(8,128)S(1)} %pad_maximum_fusion.5.pack0), channel_id=1, source_target_pairs={{0,24},{8,0},{16,8},{24,16},{1,25},{9,1},{17,9},{25,17},{2,26},{10... | collective-permute-start | bytes 491528 | tf_op jit(solution)/shard_map/ppermute | solution.py:208
  71.4 7.9 %collective-permute-start.16 = (f32[4,3,32,128]{3,2,1,0:T(8,128)S(1)}, f32[4,3,32,128]{3,2,1,0:T(8,128)S(1)}, u32[]{:S(2)}, u32[]{:S(2)}) collective-permute-start(f32[4,3,32,128]{3,2,1,0:T(8,128)S(1)} %get-tuple-element.18), channel_id=1, source_target_pairs={{0,8},{8,16},{16,24},{24,0},{1,9},{9,17},{17,25},{25,1},{2,10},{10... | collective-permute-start | bytes 589832 | tf_op jit(solution)/shard_map/ppermute | solution.py:208
  71.8 9.3 %collective-permute-start.17 = (f32[4,3,32,128]{3,2,1,0:T(8,128)S(1)}, f32[4,3,32,128]{3,2,1,0:T(8,128)S(1)}, u32[]{:S(2)}, u32[]{:S(2)}) collective-permute-start(f32[4,3,32,128]{3,2,1,0:T(8,128)S(1)} %get-tuple-element.19), channel_id=1, source_target_pairs={{0,16},{8,24},{16,0},{24,8},{1,17},{9,25},{17,1},{25,9},{2,18},{10... | collective-permute-start | bytes 589832 | tf_op jit(solution)/shard_map/ppermute | solution.py:208
  72.9 10.6 %collective-permute-start.18 = (f32[4,3,32,128]{3,2,1,0:T(8,128)S(1)}, f32[4,3,32,128]{3,2,1,0:T(8,128)S(1)}, u32[]{:S(2)}, u32[]{:S(2)}) collective-permute-start(f32[4,3,32,128]{3,2,1,0:T(8,128)S(1)} %get-tuple-element.20), channel_id=1, source_target_pairs={{0,24},{8,0},{16,8},{24,16},{1,25},{9,1},{17,9},{25,17},{2,26},{10... | collective-permute-start | bytes 589832 | tf_op jit(solution)/shard_map/ppermute | solution.py:208
  84.2 14.2 %all-to-all-start.1 = ((f32[8,3,16,128]{3,2,1,0:T(8,128)}), f32[8,3,16,128]{3,2,1,0:T(8,128)S(1)}, u32[]{:S(2)}, u32[]{:S(2)}) async-start(f32[8,3,16,128]{3,2,1,0:T(8,128)} %spread.1), calls=%async_computation.1 | async-start | bytes 393216 | tf_op jit(solution)/shard_map/all_to_all | solution.py:292
  98.4 3.7 %collective-permute-start.19 = (f32[3,16,128]{2,1,0:T(8,128)S(1)}, f32[3,16,128]{2,1,0:T(8,128)S(1)}, u32[]{:S(2)}, u32[]{:S(2)}) collective-permute-start(f32[3,16,128]{2,1,0:T(8,128)S(1)} %reduce_sum.9.share), channel_id=1, source_target_pairs={{0,192},{32,224},{64,128},{96,160},{1,193},{33,225},{65,129},{97,1... | collective-permute-start | bytes 73736 | tf_op jit(solution)/shard_map/ppermute | solution.py:293

commit v4 on v3

--- a/solution.py
+++ b/solution.py
@@ -77,20 +77,23 @@
 
 
 def solve_kernel(
-    place, pack0, pack1, pack2, pack3, left0, left1, left2, left3, outer, middle,
+    place, pack0, pack1, pack2, pack3, twin0, twin1, twin2, twin3,
+    left0, left1, left2, left3, outer, middle,
     solved_ref, part0, part1, part2, part3, diag, inv, right, partial,
 ):
-    x, owner, offset = (place[i] for i in range(3))
+    x, owner, offset, second = (place[i] for i in range(4))
     rows = lax.broadcasted_iota(jnp.int32, (32, TILE), 0)
     cols = lax.broadcasted_iota(jnp.int32, (32, TILE), 1) + offset
-    packs, lefts = (pack0, pack1, pack2, pack3), (left0, left1, left2, left3)
+    packs, twins = (pack0, pack1, pack2, pack3), (twin0, twin1, twin2, twin3)
+    lefts = (left0, left1, left2, left3)
     for step in range(4):
-        at = 0
-        for block in range(4):
-            for zl in range(block, 4):
-                start = pl.multiple_of((zl * 4 + (x - step) % 4) * 32, 32)
-                diag[block, pl.ds(start, 32), :] = packs[step][at : at + 32, :]
-                at += 32
+        for at in range(6):
+            zl, block = (at, 0) if at < 4 else (at - 2, 2)
+            to = pl.ds(pl.multiple_of((zl * 4 + (x - step) % 4) * 32, 32), 32)
+            mine = packs[step][at * 32 : (at + 1) * 32, :]
+            other = twins[step][at * 32 : (at + 1) * 32, :]
+            diag[block, to, :] = jnp.where(second == 1, other, mine)
+            diag[block + 1, to, :] = jnp.where(second == 1, mine, other)
         for zl in range(4):
             start = pl.multiple_of((zl * 4 + (x - step) % 4) * 32, 32)
             eye = (rows + start == cols).astype(jnp.float32)
@@ -262,11 +265,17 @@
     sent = near, across, lax.ppermute(both, "y", [(2, 0), (3, 1)])
     last = lines[:, 2].reshape(TILE, TILE)
     low_block, rest = own_pair(last, *over_y(last))
-    lefts = (lines, *over_x(lines))
-    quads = ordered(low_block, rest, swap(low_block), swap(rest))
-    pack = jnp.concatenate([quads[c][32 * c :] for c in range(4)], 0)
+    left1, left2 = (
+        lax.ppermute(lines, "x", [(i, (i + s) % 4) for i in range(4)]) for s in (1, 2)
+    )
+    left3 = lax.ppermute(lines, "x", [(i, (i + 3) % 4) for i in range(4)])
+    lefts = (lines, left1, left2, left3)
+    odd = lax.axis_index("y") % 2 == 1
+    high = jnp.where(odd, rest, low_block)
+    pack = jnp.concatenate([jnp.where(odd, low_block, rest), high[64:]], 0)
     packs = (pack, *over_x(pack))
-    panels = panel_blocks(both, sent, low_block)
+    twins = tuple(swap(p) for p in packs)
+    panels = panel_blocks(both, sent, lines)
     adj_panel = jnp.concatenate([p[:288] for p in panels], 1)
     fac_panel = jnp.concatenate([p[288:] for p in panels], 1)
 
@@ -284,9 +293,9 @@
     below = jnp.concatenate([f0, f1, jnp.where(owner, 0.0, f2[32:])], 1)
     outer = close_dot(weights, below, over_rows)
     place = jnp.stack(
-        [x, owner.astype(jnp.int32), col * TILE - 512]
+        [x, owner.astype(jnp.int32), col * TILE - 512, lax.axis_index("k")]
     ).astype(jnp.int32)
-    solved, *parts = solved_parts(place, *packs, *lefts, outer, middle)
+    solved, *parts = solved_parts(place, *packs, *twins, *lefts, outer, middle)
     moved = over_x(tuple(parts[1:]))
     spread = spread_sum(parts[0], *moved)
     share = lax.all_to_all(spread, ("zh", "zl"), 0, 0, tiled=True).sum(axis=0)

time: 103 us -> 101 us (0.981)
  the two profiles are of different devices: /device:TPU:6 before, /device:TPU:4 now
where the time goes in v4:
time: 101 us
  waiting for transfers between devices  51.9 us (51%)
  starting transfers between devices  31.7 us (31%)
  Pallas kernels  9.42 us (9%)
  matrix products  3.32 us (3%)
  local copies, waits for them, and re-layouts  2.24 us (2%)
  other arithmetic  1.5 us (1%)
    all_to_all x1, waiting for transfers between devices, step(): lines = lax.all_to_all(copies(factor), ('zh', 'zl'), 0, 0, tiled=True)[4:]  14.4 us
    all_to_all x1, waiting for transfers between devices, step(): share = lax.all_to_all(spread, ('zh', 'zl'), 0, 0, tiled=True).sum(axis=0)  9.61 us
    ppermute x6, waiting for transfers between devices, over_x(): lax.ppermute(b, 'x', [(i, (i + s) % 4) for i in range(4)])  9.35 us
    all_to_all x1, starting transfers between devices, step(): lines = lax.all_to_all(copies(factor), ('zh', 'zl'), 0, 0, tiled=True)[4:]  8.6 us
    pallas_call x1, Pallas kernels, solved_parts(): pl.pallas_call(solve_kernel, out_shape=(pltpu.VMEM((NB, WIDE), jnp.float3...  6.57 us
    ppermute x6, starting transfers between devices, over_x(): lax.ppermute(b, 'x', [(i, (i + s) % 4) for i in range(4)])  5.63 us
    ppermute x1, waiting for transfers between devices, over_y(): far = lax.ppermute(block, 'y', [(2, 0), (3, 1)])  5.35 us
    ppermute x1, waiting for transfers between devices, step(): left3 = lax.ppermute(lines, 'x', [(i, (i + 3) % 4) for i in range(4)])  4.95 us
  transfers between devices with their start and end apart: 24, of which 10 were waited for; matrix products, arithmetic and copies ran while one was open for 5% of the time, Pallas kernels for 2%

profile of v4, /device:TPU:4, one launch (start us, length us, event | category | flops | bytes accessed | tf_op | source)
XLA Modules:
  0.0 100.6 jit_solution(3166348770357729522)
XLA Ops:
  0.0 1.0 slice.123
  1.0 0.9 slice.122
  2.0 0.1 bitcast_select_fusion
  2.1 1.3 %collective-permute-start = (f32[576,128]{1,0:T(8,128)S(1)}, f32[576,128]{1,0:T(8,128)S(1)}, u32[]{:S(2)}, u32[]{:S(2)}) collective-permute-start(f32[576,128]{1,0:T(8,128)S(1)} %pad_maximum_fusion.4), channel_id=1, source_target_pairs={{4,2},{6,0},{5,3},{7,1},{12,10},{14,8},{13,11},{15,9},{20,18},{22,... | collective-permute-start | bytes 884744 | tf_op jit(solution)/shard_map/ppermute | solution.py:263
  3.4 0.7 collective-permute-start.1
  4.0 1.3 %collective-permute-start.2 = (f32[576,128]{1,0:T(8,128)S(1)}, f32[576,128]{1,0:T(8,128)S(1)}, u32[]{:S(2)}, u32[]{:S(2)}) collective-permute-start(f32[576,128]{1,0:T(8,128)S(1)} %pad_maximum_fusion.4), channel_id=1, source_target_pairs={{4,0},{6,2},{5,1},{7,3},{12,8},{14,10},{13,9},{15,11},{20,16},{22,... | collective-permute-start | bytes 884744 | tf_op jit(solution)/shard_map/ppermute | solution.py:265
  5.3 1.6 %copies.1 = f32[8,3,32,128]{3,2,1,0:T(8,128)} custom-call(f32[9,3,32,128]{3,2,1,0:T(8,128)} %bitcast.30), custom_call_target="tpu_custom_call" | custom-call | tf_op jit(solution)/shard_map/copies/pallas_call | solution.py:197
  6.9 8.6 %all-to-all-start = ((f32[8,3,32,128]{3,2,1,0:T(8,128)}), f32[8,3,32,128]{3,2,1,0:T(8,128)S(1)}, u32[]{:S(2)}, u32[]{:S(2)}) async-start(f32[8,3,32,128]{3,2,1,0:T(8,128)} %copies.1), calls=%async_computation | async-start | bytes 786432 | tf_op jit(solution)/shard_map/all_to_all | solution.py:261
  15.5 0.1 bitcast_select_fusion.1
  15.6 0.1 pad_add_fusion.place
  15.7 0.1 pad_add_fusion.1.place
  15.8 14.4 %all-to-all-done = f32[8,3,32,128]{3,2,1,0:T(8,128)S(1)} async-done(((f32[8,3,32,128]{3,2,1,0:T(8,128)}), f32[8,3,32,128]{3,2,1,0:T(8,128)S(1)}, u32[]{:S(2)}, u32[]{:S(2)}) %all-to-all-start) | async-done | bytes 393248 | tf_op jit(solution)/shard_map/all_to_all | solution.py:261
  30.2 1.3 %collective-permute-start.7 = (f32[128,128]{1,0:T(8,128)S(1)}, f32[128,128]{1,0:T(8,128)S(1)}, u32[]{:S(2)}, u32[]{:S(2)}) collective-permute-start(f32[128,128]{1,0:T(8,128)S(1)} %bitcast.47), channel_id=1, source_target_pairs={{4,0},{6,2},{5,1},{7,3},{12,8},{14,10},{13,9},{15,11},{20,16},{22,... | collective-permute-start | bytes 196616 | tf_op jit(solution)/shard_map/ppermute | solution.py:219
  31.5 0.7 collective-permute-start.5
  32.2 1.3 %collective-permute-start.6 = (f32[128,128]{1,0:T(8,128)S(1)}, f32[128,128]{1,0:T(8,128)S(1)}, u32[]{:S(2)}, u32[]{:S(2)}) collective-permute-start(f32[128,128]{1,0:T(8,128)S(1)} %bitcast.49), channel_id=1, source_target_pairs={{4,2},{6,0},{5,3},{7,1},{12,10},{14,8},{13,11},{15,9},{20,18},{22,... | collective-permute-start | bytes 196616 | tf_op jit(solution)/shard_map/ppermute | solution.py:217
  33.5 1.3 %collective-permute-start.15 = (f32[4,3,32,128]{3,2,1,0:T(8,128)S(1)}, f32[4,3,32,128]{3,2,1,0:T(8,128)S(1)}, u32[]{:S(2)}, u32[]{:S(2)}) collective-permute-start(f32[4,3,32,128]{3,2,1,0:T(8,128)S(1)} %slice.124.left0), channel_id=1, source_target_pairs={{0,8},{8,16},{16,24},{24,0},{1,9},{9,17},{17,25},{25,1},{2,10},{10... | collective-permute-start | bytes 589832 | tf_op jit(solution)/shard_map/ppermute | solution.py:269
  34.8 0.1 collective-permute-start.3
  35.0 5.3 %collective-permute-done.7 = f32[128,128]{1,0:T(8,128)S(1)} collective-permute-done((f32[128,128]{1,0:T(8,128)S(1)}, f32[128,128]{1,0:T(8,128)S(1)}, u32[]{:S(2)}, u32[]{:S(2)}) %collective-permute-start.7) | collective-permute-done | bytes 65568 | tf_op jit(solution)/shard_map/ppermute | solution.py:219
  40.3 3.2 %collective-permute-done.6 = f32[128,128]{1,0:T(8,128)S(1)} collective-permute-done((f32[128,128]{1,0:T(8,128)S(1)}, f32[128,128]{1,0:T(8,128)S(1)}, u32[]{:S(2)}, u32[]{:S(2)}) %collective-permute-start.6) | collective-permute-done | bytes 65568 | tf_op jit(solution)/shard_map/ppermute | solution.py:217
  43.6 1.3 %collective-permute-start.8 = (f32[192,128]{1,0:T(8,128)S(1)}, f32[192,128]{1,0:T(8,128)S(1)}, u32[]{:S(2)}, u32[]{:S(2)}) collective-permute-start(f32[192,128]{1,0:T(8,128)S(1)} %pad_maximum_fusion.5.pack0), channel_id=1, source_target_pairs={{0,8},{8,16},{16,24},{24,0},{1,9},{9,17},{17,25},{25,1},{2,10},{10... | collective-permute-start | bytes 294920 | tf_op jit(solution)/shard_map/ppermute | solution.py:211
  44.9 0.8 collective-permute-start.9
  45.7 1.1 %collective-permute-start.10 = (f32[192,128]{1,0:T(8,128)S(1)}, f32[192,128]{1,0:T(8,128)S(1)}, u32[]{:S(2)}, u32[]{:S(2)}) collective-permute-start(f32[192,128]{1,0:T(8,128)S(1)} %pad_maximum_fusion.5.pack0), channel_id=1, source_target_pairs={{0,24},{8,0},{16,8},{24,16},{1,25},{9,1},{17,9},{25,17},{2,26},{10... | collective-permute-start | bytes 294920 | tf_op jit(solution)/shard_map/ppermute | solution.py:211
  46.8 0.1 broadcast_select_fusion.9
  47.2 1.0 %fusion.2 = f32[512,512]{1,0:T(8,128)S(1)} fusion(f32[256,512]{1,0:T(8,128)S(1)} %slice.129, f32[32,512]{1,0:T(8,128)S(1)} %maximum_multiply_fusion, f32[288,128]{1,0:T(8,128)S(1)} %get-tuple-element.44, f32[288,128]{1,0:T(8,128)S(1)} %get-tuple-element.35, f32[288,128]{1,0:T(8,128)S(1)} %get-tuple-element.42, f32[288,128]{1,0:T(8,128)S(1)} %get-tuple-element.31, ...), kind=kOutput, calls=%fused_computation.10 | convolution fusion | flops 454459392 | bytes 2293760 | tf_op jit(solution)/shard_map/dot_general | solution.py:16
  48.2 1.1 %fusion.middle = f32[512,512]{1,0:T(8,128)S(1)} fusion(f32[512,512]{1,0:T(8,128)S(1)} %fusion.2, f32[256,512]{1,0:T(8,128)S(1)} %slice.129, f32[32,512]{1,0:T(8,128)S(1)} %maximum_multiply_fusion, f32[288,128]{1,0:T(8,128)S(1)} %get-tuple-element.44, f32[288,128]{1,0:T(8,128)S(1)} %get-tuple-element.35, f32[288,128]{1,0:T(8,128)S(1)} %get-tuple-element.42, ...), kind=kOutput, calls=%fused_computation.1 | convolution fusion | flops 455245824 | bytes 3342336 | tf_op jit(solution)/shard_map/dot_general | solution.py:16
  49.3 3.1 %collective-permute-start.16 = (f32[4,3,32,128]{3,2,1,0:T(8,128)S(1)}, f32[4,3,32,128]{3,2,1,0:T(8,128)S(1)}, u32[]{:S(2)}, u32[]{:S(2)}) collective-permute-start(f32[4,3,32,128]{3,2,1,0:T(8,128)S(1)} %slice.124.left0), channel_id=1, source_target_pairs={{0,16},{8,24},{16,0},{24,8},{1,17},{9,25},{17,1},{25,9},{2,18},{10... | collective-permute-start | bytes 589832 | tf_op jit(solution)/shard_map/ppermute | solution.py:269
  52.4 0.3 collective-permute-start.12
  52.7 0.3 collective-permute-start.13
  53.0 0.3 collective-permute-start.14
  53.3 0.6 fusion.3.outer
  53.9 4.3 %collective-permute-done.16.left2 = f32[4,3,32,128]{3,2,1,0:T(8,128)S(1)} collective-permute-done((f32[4,3,32,128]{3,2,1,0:T(8,128)S(1)}, f32[4,3,32,128]{3,2,1,0:T(8,128)S(1)}, u32[]{:S(2)}, u32[]{:S(2)}) %collective-permute-start.16) | collective-permute-done | bytes 196640 | tf_op jit(solution)/shard_map/ppermute | solution.py:269
  58.2 4.9 %collective-permute-done.17.left3 = f32[4,3,32,128]{3,2,1,0:T(8,128)S(1)} collective-permute-done((f32[4,3,32,128]{3,2,1,0:T(8,128)S(1)}, f32[4,3,32,128]{3,2,1,0:T(8,128)S(1)}, u32[]{:S(2)}, u32[]{:S(2)}) %collective-permute-start.17) | collective-permute-done | bytes 196640 | tf_op jit(solution)/shard_map/ppermute | solution.py:271
  63.1 6.6 %solve.1 = (f32[512,384]{1,0:T(8,128)S(1)}, f32[4,3,32,128]{3,2,1,0:T(8,128)S(1)}, f32[4,3,32,128]{3,2,1,0:T(8,128)S(1)}, f32[4,3,32,128]{3,2,1,0:T(8,128)S(1)}, f32[4,3,32,128]{3,2,1,0:T(8,128)S(1)}) custom-call(s32[4]{0:T(128)S(1)} %pad_add_fusion.1.place, f32[192,128]{1,0:T(8,128)S(1)} %pad_maximum_fusion.5.pack0, ...), custom_call_target="tpu_custom_call" | custom-call | tf_op jit(solution)/shard_map/solve/pallas_call | solution.py:173
  69.7 0.4 collective-permute-start.18
  70.1 1.9 %collective-permute-start.19 = (f32[4,3,32,128]{3,2,1,0:T(8,128)S(1)}, f32[4,3,32,128]{3,2,1,0:T(8,128)S(1)}, u32[]{:S(2)}, u32[]{:S(2)}) collective-permute-start(f32[4,3,32,128]{3,2,1,0:T(8,128)S(1)} %get-tuple-element.19), channel_id=1, source_target_pairs={{0,16},{8,24},{16,0},{24,8},{1,17},{9,25},{17,1},{25,9},{2,18},{10... | collective-permute-start | bytes 589832 | tf_op jit(solution)/shard_map/ppermute | solution.py:211
  72.1 0.1 collective-permute-start.20
  72.1 0.6 fusion.18
  72.8 0.2 reshape.70
  73.0 4.4 %collective-permute-done.18.part1 = f32[4,3,32,128]{3,2,1,0:T(8,128)S(1)} collective-permute-done((f32[4,3,32,128]{3,2,1,0:T(8,128)S(1)}, f32[4,3,32,128]{3,2,1,0:T(8,128)S(1)}, u32[]{:S(2)}, u32[]{:S(2)}) %collective-permute-start.18) | collective-permute-done | bytes 196640 | tf_op jit(solution)/shard_map/ppermute | solution.py:211
  77.3 3.4 %collective-permute-done.19.part2 = f32[4,3,32,128]{3,2,1,0:T(8,128)S(1)} collective-permute-done((f32[4,3,32,128]{3,2,1,0:T(8,128)S(1)}, f32[4,3,32,128]{3,2,1,0:T(8,128)S(1)}, u32[]{:S(2)}, u32[]{:S(2)}) %collective-permute-start.19) | collective-permute-done | bytes 196640 | tf_op jit(solution)/shard_map/ppermute | solution.py:211
  80.7 1.6 %collective-permute-done.20.part3 = f32[4,3,32,128]{3,2,1,0:T(8,128)S(1)} collective-permute-done((f32[4,3,32,128]{3,2,1,0:T(8,128)S(1)}, f32[4,3,32,128]{3,2,1,0:T(8,128)S(1)}, u32[]{:S(2)}, u32[]{:S(2)}) %collective-permute-start.20) | collective-permute-done | bytes 196640 | tf_op jit(solution)/shard_map/ppermute | solution.py:211
  82.3 0.7 spread.1
  83.0 3.4 %all-to-all-start.1 = ((f32[8,3,16,128]{3,2,1,0:T(8,128)}), f32[8,3,16,128]{3,2,1,0:T(8,128)S(1)}, u32[]{:S(2)}, u32[]{:S(2)}) async-start(f32[8,3,16,128]{3,2,1,0:T(8,128)} %spread.1), calls=%async_computation.1 | async-start | bytes 393216 | tf_op jit(solution)/shard_map/all_to_all | solution.py:301
  86.5 9.6 %all-to-all-done.1 = f32[8,3,16,128]{3,2,1,0:T(8,128)S(1)} async-done(((f32[8,3,16,128]{3,2,1,0:T(8,128)}), f32[8,3,16,128]{3,2,1,0:T(8,128)S(1)}, u32[]{:S(2)}, u32[]{:S(2)}) %all-to-all-start.1) | async-done | bytes 196640 | tf_op jit(solution)/shard_map/all_to_all | solution.py:301
  96.1 2.2 %collective-permute-start.21 = (f32[3,16,128]{2,1,0:T(8,128)S(1)}, f32[3,16,128]{2,1,0:T(8,128)S(1)}, u32[]{:S(2)}, u32[]{:S(2)}) collective-permute-start(f32[3,16,128]{2,1,0:T(8,128)S(1)} %reduce_sum.9.share), channel_id=1, source_target_pairs={{0,192},{32,224},{64,128},{96,160},{1,193},{33,225},{65,129},{97,1... | collective-permute-start | bytes 73736 | tf_op jit(solution)/shard_map/ppermute | solution.py:302
  98.3 0.8 maximum_maximum_fusion.base
  99.1 0.7 collective-permute-done.21.other
  99.9 0.6 finish.1
  (44 shorter events, 0.5 us)
Async XLA Ops:
  0.0 2.0 %copy-start.1 = (f32[9,32,3,128]{3,1,2,0:T(8,128)S(1)}, f32[9,32,3,128]{3,1,2,0:T(8,128)}, u32[]{:S(2)}) copy-start(f32[9,32,3,128]{3,1,2,0:T(8,128)} %param.3) | copy-start | bytes 1327108
  2.1 30.1 %collective-permute-start = (f32[576,128]{1,0:T(8,128)S(1)}, f32[576,128]{1,0:T(8,128)S(1)}, u32[]{:S(2)}, u32[]{:S(2)}) collective-permute-start(f32[576,128]{1,0:T(8,128)S(1)} %pad_maximum_fusion.4), channel_id=1, source_target_pairs={{4,2},{6,0},{5,3},{7,1},{12,10},{14,8},{13,11},{15,9},{20,18},{22,... | collective-permute-start | bytes 884744 | tf_op jit(solution)/shard_map/ppermute | solution.py:263
  3.4 30.1 %collective-permute-start.1 = (f32[576,128]{1,0:T(8,128)S(1)}, f32[576,128]{1,0:T(8,128)S(1)}, u32[]{:S(2)}, u32[]{:S(2)}) collective-permute-start(f32[576,128]{1,0:T(8,128)S(1)} %pad_maximum_fusion.4), channel_id=1, source_target_pairs={{4,6},{6,4},{5,7},{7,5},{12,14},{14,12},{13,15},{15,13},{20,22},{2... | collective-permute-start | bytes 884744 | tf_op jit(solution)/shard_map/ppermute | solution.py:264
  4.0 30.7 %collective-permute-start.2 = (f32[576,128]{1,0:T(8,128)S(1)}, f32[576,128]{1,0:T(8,128)S(1)}, u32[]{:S(2)}, u32[]{:S(2)}) collective-permute-start(f32[576,128]{1,0:T(8,128)S(1)} %pad_maximum_fusion.4), channel_id=1, source_target_pairs={{4,0},{6,2},{5,1},{7,3},{12,8},{14,10},{13,9},{15,11},{20,16},{22,... | collective-permute-start | bytes 884744 | tf_op jit(solution)/shard_map/ppermute | solution.py:265
  6.9 8.8 %copy-start = (f32[9,32,3,128]{3,1,2,0:T(8,128)S(1)}, f32[9,32,3,128]{3,1,2,0:T(8,128)}, u32[]{:S(2)}) copy-start(f32[9,32,3,128]{3,1,2,0:T(8,128)} %param.2) | copy-start | bytes 1327108
  6.9 23.3 %all-to-all-start = ((f32[8,3,32,128]{3,2,1,0:T(8,128)}), f32[8,3,32,128]{3,2,1,0:T(8,128)S(1)}, u32[]{:S(2)}, u32[]{:S(2)}) async-start(f32[8,3,32,128]{3,2,1,0:T(8,128)} %copies.1), calls=%async_computation | async-start | bytes 786432 | tf_op jit(solution)/shard_map/all_to_all | solution.py:261
  30.2 10.1 %collective-permute-start.7 = (f32[128,128]{1,0:T(8,128)S(1)}, f32[128,128]{1,0:T(8,128)S(1)}, u32[]{:S(2)}, u32[]{:S(2)}) collective-permute-start(f32[128,128]{1,0:T(8,128)S(1)} %bitcast.47), channel_id=1, source_target_pairs={{4,0},{6,2},{5,1},{7,3},{12,8},{14,10},{13,9},{15,11},{20,16},{22,... | collective-permute-start | bytes 196616 | tf_op jit(solution)/shard_map/ppermute | solution.py:219
  31.5 8.8 %collective-permute-start.5 = (f32[128,128]{1,0:T(8,128)S(1)}, f32[128,128]{1,0:T(8,128)S(1)}, u32[]{:S(2)}, u32[]{:S(2)}) collective-permute-start(f32[128,128]{1,0:T(8,128)S(1)} %bitcast.48), channel_id=1, source_target_pairs={{4,6},{6,4},{5,7},{7,5},{12,14},{14,12},{13,15},{15,13},{20,22},{2... | collective-permute-start | bytes 196616 | tf_op jit(solution)/shard_map/ppermute | solution.py:218
  32.2 11.3 %collective-permute-start.6 = (f32[128,128]{1,0:T(8,128)S(1)}, f32[128,128]{1,0:T(8,128)S(1)}, u32[]{:S(2)}, u32[]{:S(2)}) collective-permute-start(f32[128,128]{1,0:T(8,128)S(1)} %bitcast.49), channel_id=1, source_target_pairs={{4,2},{6,0},{5,3},{7,1},{12,10},{14,8},{13,11},{15,9},{20,18},{22,... | collective-permute-start | bytes 196616 | tf_op jit(solution)/shard_map/ppermute | solution.py:217
  33.5 19.5 %collective-permute-start.15 = (f32[4,3,32,128]{3,2,1,0:T(8,128)S(1)}, f32[4,3,32,128]{3,2,1,0:T(8,128)S(1)}, u32[]{:S(2)}, u32[]{:S(2)}) collective-permute-start(f32[4,3,32,128]{3,2,1,0:T(8,128)S(1)} %slice.124.left0), channel_id=1, source_target_pairs={{0,8},{8,16},{16,24},{24,0},{1,9},{9,17},{17,25},{25,1},{2,10},{10... | collective-permute-start | bytes 589832 | tf_op jit(solution)/shard_map/ppermute | solution.py:269
  34.8 10.8 %collective-permute-start.3 = (f32[576,128]{1,0:T(8,128)S(1)}, f32[576,128]{1,0:T(8,128)S(1)}, u32[]{:S(2)}, u32[]{:S(2)}) collective-permute-start(f32[576,128]{1,0:T(8,128)S(1)} %broadcast_select_fusion.1), channel_id=1, source_target_pairs={{0,1},{1,0},{2,3},{3,2},{4,5},{5,4},{6,7},{7,6},{8,9},{9,8},{10,11... | collective-permute-start | bytes 884744 | tf_op jit(solution)/shard_map/ppermute | solution.py:229
  40.3 6.5 %collective-permute-start.4 = (f32[576,128]{1,0:T(8,128)S(1)}, f32[576,128]{1,0:T(8,128)S(1)}, u32[]{:S(2)}, u32[]{:S(2)}) collective-permute-start(f32[576,128]{1,0:T(8,128)S(1)} %broadcast_select_fusion), channel_id=1, source_target_pairs={{0,1},{1,0},{2,3},{3,2},{4,5},{5,4},{6,7},{7,6},{8,9},{9,8},{10,11... | collective-permute-start | bytes 884744 | tf_op jit(solution)/shard_map/ppermute | solution.py:229
  43.6 5.7 %collective-permute-start.8 = (f32[192,128]{1,0:T(8,128)S(1)}, f32[192,128]{1,0:T(8,128)S(1)}, u32[]{:S(2)}, u32[]{:S(2)}) collective-permute-start(f32[192,128]{1,0:T(8,128)S(1)} %pad_maximum_fusion.5.pack0), channel_id=1, source_target_pairs={{0,8},{8,16},{16,24},{24,0},{1,9},{9,17},{17,25},{25,1},{2,10},{10... | collective-permute-start | bytes 294920 | tf_op jit(solution)/shard_map/ppermute | solution.py:211
  44.9 7.5 %collective-permute-start.9 = (f32[192,128]{1,0:T(8,128)S(1)}, f32[192,128]{1,0:T(8,128)S(1)}, u32[]{:S(2)}, u32[]{:S(2)}) collective-permute-start(f32[192,128]{1,0:T(8,128)S(1)} %pad_maximum_fusion.5.pack0), channel_id=1, source_target_pairs={{0,16},{8,24},{16,0},{24,8},{1,17},{9,25},{17,1},{25,9},{2,18},{10... | collective-permute-start | bytes 294920 | tf_op jit(solution)/shard_map/ppermute | solution.py:211
  45.7 6.7 %collective-permute-start.10 = (f32[192,128]{1,0:T(8,128)S(1)}, f32[192,128]{1,0:T(8,128)S(1)}, u32[]{:S(2)}, u32[]{:S(2)}) collective-permute-start(f32[192,128]{1,0:T(8,128)S(1)} %pad_maximum_fusion.5.pack0), channel_id=1, source_target_pairs={{0,24},{8,0},{16,8},{24,16},{1,25},{9,1},{17,9},{25,17},{2,26},{10... | collective-permute-start | bytes 294920 | tf_op jit(solution)/shard_map/ppermute | solution.py:211
  46.8 5.9 %collective-permute-start.11 = (f32[192,128]{1,0:T(8,128)S(1)}, f32[192,128]{1,0:T(8,128)S(1)}, u32[]{:S(2)}, u32[]{:S(2)}) collective-permute-start(f32[192,128]{1,0:T(8,128)S(1)} %pad_maximum_fusion.5.pack0), channel_id=1, source_target_pairs={{0,1},{1,0},{2,3},{3,2},{4,5},{5,4},{6,7},{7,6},{8,9},{9,8},{10,11... | collective-permute-start | bytes 294920 | tf_op jit(solution)/shard_map/ppermute | solution.py:229
  49.3 8.9 %collective-permute-start.16 = (f32[4,3,32,128]{3,2,1,0:T(8,128)S(1)}, f32[4,3,32,128]{3,2,1,0:T(8,128)S(1)}, u32[]{:S(2)}, u32[]{:S(2)}) collective-permute-start(f32[4,3,32,128]{3,2,1,0:T(8,128)S(1)} %slice.124.left0), channel_id=1, source_target_pairs={{0,16},{8,24},{16,0},{24,8},{1,17},{9,25},{17,1},{25,9},{2,18},{10... | collective-permute-start | bytes 589832 | tf_op jit(solution)/shard_map/ppermute | solution.py:269
  52.4 10.7 %collective-permute-start.17 = (f32[4,3,32,128]{3,2,1,0:T(8,128)S(1)}, f32[4,3,32,128]{3,2,1,0:T(8,128)S(1)}, u32[]{:S(2)}, u32[]{:S(2)}) collective-permute-start(f32[4,3,32,128]{3,2,1,0:T(8,128)S(1)} %slice.124.left0), channel_id=1, source_target_pairs={{0,24},{8,0},{16,8},{24,16},{1,25},{9,1},{17,9},{25,17},{2,26},{10... | collective-permute-start | bytes 589832 | tf_op jit(solution)/shard_map/ppermute | solution.py:271
  52.4 10.7 %collective-permute-start.12 = (f32[192,128]{1,0:T(8,128)S(1)}, f32[192,128]{1,0:T(8,128)S(1)}, u32[]{:S(2)}, u32[]{:S(2)}) collective-permute-start(f32[192,128]{1,0:T(8,128)S(1)} %collective-permute-done.8.pack1), channel_id=1, source_target_pairs={{0,1},{1,0},{2,3},{3,2},{4,5},{5,4},{6,7},{7,6},{8,9},{9,8},{10,11... | collective-permute-start | bytes 294920 | tf_op jit(solution)/shard_map/ppermute | solution.py:229
  52.7 10.4 %collective-permute-start.13 = (f32[192,128]{1,0:T(8,128)S(1)}, f32[192,128]{1,0:T(8,128)S(1)}, u32[]{:S(2)}, u32[]{:S(2)}) collective-permute-start(f32[192,128]{1,0:T(8,128)S(1)} %collective-permute-done.9.pack2), channel_id=1, source_target_pairs={{0,1},{1,0},{2,3},{3,2},{4,5},{5,4},{6,7},{7,6},{8,9},{9,8},{10,11... | collective-permute-start | bytes 294920 | tf_op jit(solution)/shard_map/ppermute | solution.py:229
  53.0 10.1 %collective-permute-start.14 = (f32[192,128]{1,0:T(8,128)S(1)}, f32[192,128]{1,0:T(8,128)S(1)}, u32[]{:S(2)}, u32[]{:S(2)}) collective-permute-start(f32[192,128]{1,0:T(8,128)S(1)} %collective-permute-done.10.pack3), channel_id=1, source_target_pairs={{0,1},{1,0},{2,3},{3,2},{4,5},{5,4},{6,7},{7,6},{8,9},{9,8},{10,11... | collective-permute-start | bytes 294920 | tf_op jit(solution)/shard_map/ppermute | solution.py:229
  69.7 7.6 %collective-permute-start.18 = (f32[4,3,32,128]{3,2,1,0:T(8,128)S(1)}, f32[4,3,32,128]{3,2,1,0:T(8,128)S(1)}, u32[]{:S(2)}, u32[]{:S(2)}) collective-permute-start(f32[4,3,32,128]{3,2,1,0:T(8,128)S(1)} %get-tuple-element.18), channel_id=1, source_target_pairs={{0,8},{8,16},{16,24},{24,0},{1,9},{9,17},{17,25},{25,1},{2,10},{10... | collective-permute-start | bytes 589832 | tf_op jit(solution)/shard_map/ppermute | solution.py:211
  70.1 10.6 %collective-permute-start.19 = (f32[4,3,32,128]{3,2,1,0:T(8,128)S(1)}, f32[4,3,32,128]{3,2,1,0:T(8,128)S(1)}, u32[]{:S(2)}, u32[]{:S(2)}) collective-permute-start(f32[4,3,32,128]{3,2,1,0:T(8,128)S(1)} %get-tuple-element.19), channel_id=1, source_target_pairs={{0,16},{8,24},{16,0},{24,8},{1,17},{9,25},{17,1},{25,9},{2,18},{10... | collective-permute-start | bytes 589832 | tf_op jit(solution)/shard_map/ppermute | solution.py:211
  72.1 10.2 %collective-permute-start.20 = (f32[4,3,32,128]{3,2,1,0:T(8,128)S(1)}, f32[4,3,32,128]{3,2,1,0:T(8,128)S(1)}, u32[]{:S(2)}, u32[]{:S(2)}) collective-permute-start(f32[4,3,32,128]{3,2,1,0:T(8,128)S(1)} %get-tuple-element.20), channel_id=1, source_target_pairs={{0,24},{8,0},{16,8},{24,16},{1,25},{9,1},{17,9},{25,17},{2,26},{10... | collective-permute-start | bytes 589832 | tf_op jit(solution)/shard_map/ppermute | solution.py:211
  83.0 13.1 %all-to-all-start.1 = ((f32[8,3,16,128]{3,2,1,0:T(8,128)}), f32[8,3,16,128]{3,2,1,0:T(8,128)S(1)}, u32[]{:S(2)}, u32[]{:S(2)}) async-start(f32[8,3,16,128]{3,2,1,0:T(8,128)} %spread.1), calls=%async_computation.1 | async-start | bytes 393216 | tf_op jit(solution)/shard_map/all_to_all | solution.py:301
  96.1 3.7 %collective-permute-start.21 = (f32[3,16,128]{2,1,0:T(8,128)S(1)}, f32[3,16,128]{2,1,0:T(8,128)S(1)}, u32[]{:S(2)}, u32[]{:S(2)}) collective-permute-start(f32[3,16,128]{2,1,0:T(8,128)S(1)} %reduce_sum.9.share), channel_id=1, source_target_pairs={{0,192},{32,224},{64,128},{96,160},{1,193},{33,225},{65,129},{97,1... | collective-permute-start | bytes 73736 | tf_op jit(solution)/shard_map/ppermute | solution.py:302
